TPU v7x, 32 devices: a whole 2x2x4 slice. The times are simulated.
32 devices in a mesh: row: 8 (over y, x, core), col: 4 (over z).
Axes of the slice: x: 2, y: 2, z: 4, core: 2. Of those that a mesh axis runs over, the one named last changes fastest.
Arguments:
- right_side: float32 [2, 2048, 1024], P(None, 'row', 'col'), may hold values from -6 to 6
- probe: float32 [2, 256, 256], replicated, may hold values from -6 to 6
- detector_weights: float32 [256, 256], replicated, may hold values from 0.1 to 10
- offsets: int32 [8, 4, 4, 2], P('row', 'col'), may hold values from -128 to 127, as said below
- counts: int32 [8, 4], P('row', 'col'), may hold values from 2 to 4, as said below
Outputs:
- solution_field: float32 [2, 2048, 1024], P(None, 'row', 'col')
- residual: float32 [2, 2048, 1024], P(None, 'row', 'col')
Inputs may be any that keep to these rules, and one draw needn't show every extreme that they name: `counts`: every region holds at least two positions; in every draw some region holds exactly 4. In every region slot 0 has both offsets negative and slot 1 both offsets non-negative.
All inputs are finite; a program needn't handle non-finite values.
Results may differ from a plain program's by a relative error of at most 0.0003.
Values sent between devices are 32-bit elements; how exact they have to be, the bound alone decides.
A program may use at most 64 MiB of HBM per device.

v0:
```python
import functools
import math

import jax
import jax.numpy as jnp
import numpy as np
from jax import lax
from jax.experimental import pallas as pl
from jax.experimental.pallas import tpu as pltpu
from jax.sharding import PartitionSpec as P

ITERS = 3
RIDGE = 0.5
MESH = pl.DeviceIdType.MESH
F32 = jnp.float32
BF16 = jnp.bfloat16


def tables(length):
    half = length // 2
    k = np.arange(half)[:, None]
    n = np.arange(half)[None, :]
    out = []
    for odd in (0, 1):
        angle = 2.0 * math.pi * ((n * (2 * k + odd)) % length) / length
        re, im = np.cos(angle) / math.sqrt(length), -np.sin(angle) / math.sqrt(length)
        real = np.block([[re, -im], [im, re]])
        for mat in (real, real.T):
            hi = mat.astype(BF16)
            out += [hi, (mat - hi.astype(np.float64)).astype(BF16)]
    return np.stack(out)


def kernel(
    n_row, n_col, cap, side,
    off_ref, cnt_ref, rhs_ref, probe_ref, w_ref, mat_ref,
    sol_ref, res_ref,
    R, G, L, S, D, PR, X, Y, W, RA, CA, CC, RC, T1, T2,
    bar_send, bar_recv, s1_send, s1_recv, s2_send, s2_recv,
):
    h = side // 2
    own = slice(h, h + side)
    row = lax.axis_index("row")
    col = lax.axis_index("col")

    def chunks(total, step, body):
        def run(i, carry):
            body(pl.ds(pl.multiple_of(i * step, step), step), i * step)
            return carry
        lax.fori_loop(0, total // step, run, 0)

    def clear(rows, _):
        G[:, rows, :] = jnp.zeros((2, 32, 2 * side), F32)
    chunks(2 * side, 32, clear)

    for buf in (RA, CA, CC, RC):
        def clear_b(rows, _, buf=buf):
            buf[:, rows, :] = jnp.zeros((2, 32, buf.shape[2]), F32)
        chunks(buf.shape[1], 32, clear_b)
    G[:, own, own] = rhs_ref[...]

    barrier = pltpu.get_barrier_semaphore()
    for d in range(1, n_row):
        pl.semaphore_signal(barrier, inc=1, device_id=(lax.rem(row + d, n_row), col), device_id_type=MESH)
    for d in range(1, n_col):
        pl.semaphore_signal(barrier, inc=1, device_id=(row, lax.rem(col + d, n_col)), device_id_type=MESH)
    pl.semaphore_wait(barrier, n_row - 1 + n_col - 1)

    def both(index, low_src, low_dst, high_src, high_dst, axis):
        at, count = (row, n_row) if axis == 0 else (col, n_col)

        def target(step):
            return (row + step, col) if axis == 0 else (row, col + step)

        low = pltpu.make_async_remote_copy(
            src_ref=low_src, dst_ref=low_dst, send_sem=bar_send.at[2 * index], recv_sem=bar_recv.at[2 * index],
            device_id=target(-1), device_id_type=MESH)
        high = pltpu.make_async_remote_copy(
            src_ref=high_src, dst_ref=high_dst, send_sem=bar_send.at[2 * index + 1],
            recv_sem=bar_recv.at[2 * index + 1], device_id=target(1), device_id_type=MESH)

        def start():
            pl.when(at > 0)(low.start)
            pl.when(at < count - 1)(high.start)

        def wait():
            @pl.when(at > 0)
            def _():
                low.wait_send()
                high.wait_recv()

            @pl.when(at < count - 1)
            def _():
                high.wait_send()
                low.wait_recv()

        return start, wait

    edges = (slice(0, h), slice(3 * h, 4 * h))
    one, two, top_h, end_h = slice(h, 2 * h), slice(2 * h, 3 * h), slice(0, h), slice(3 * h, 4 * h)

    def gather():
        re_turn = both(8, G.at[0, own, one], G.at[0, own, end_h], G.at[0, own, two], G.at[0, own, top_h], 1)
        im_turn = both(9, G.at[1, one, own], G.at[1, end_h, own], G.at[1, two, own], G.at[1, top_h, own], 0)
        rest = [
            both(10, G.at[0, one, own], G.at[0, end_h, own], G.at[0, two, own], G.at[0, top_h, own], 0),
            both(11, G.at[1, own, one], G.at[1, own, end_h], G.at[1, own, two], G.at[1, own, top_h], 1),
        ]
        for start, _ in (re_turn, im_turn, *rest):
            start()
        re_turn[1]()
        for q, e in enumerate(edges):
            rest.append(both(12 + q, G.at[0, one, e], G.at[0, end_h, e], G.at[0, two, e], G.at[0, top_h, e], 0))
            rest[-1][0]()
        im_turn[1]()
        for q, e in enumerate(edges):
            rest.append(both(14 + q, G.at[1, e, one], G.at[1, e, end_h], G.at[1, e, two], G.at[1, e, top_h], 1))
            rest[-1][0]()

        def wait():
            for _, done in rest:
                done()

        return wait

    gather_wait = gather()

    for s in range(cap):
        on = jnp.where(s < cnt_ref[0], 1.0, 0.0).astype(F32)
        for c in range(2):
            rolled = pltpu.roll(probe_ref[c], off_ref[2 * s] + h, 0)
            PR[s, c] = pltpu.roll(rolled, off_ref[2 * s + 1] + h, 1) * on

    def three(val):
        top = val.astype(BF16)
        rest = val - top.astype(F32)
        mid = rest.astype(BF16)
        return top, mid, (rest - mid.astype(F32)).astype(BF16)

    first = lax.broadcasted_iota(jnp.int32, (side, side), 0)
    second = lax.broadcasted_iota(jnp.int32, (side, side), 1)
    freq = jnp.where(first >= h, 2 * (first - h) + 1, 2 * first)
    pick = jnp.where(second == freq, 1.0, 0.0).astype(BF16)
    by_row = sum(jnp.dot(pick, part, preferred_element_type=F32) for part in three(w_ref[...]))
    parts = three(by_row)
    lane = jnp.where(second >= h, second - h, second)
    for q in range(2):
        pick = jnp.where(first == 2 * lane + q, 1.0, 0.0).astype(BF16)
        W[q] = sum(jnp.dot(part, pick, preferred_element_type=F32) for part in parts)

    def clear_s(rows, _):
        S[:, rows, :] = jnp.zeros((2, 32, 2 * side), F32)
    chunks(2 * side, 32, clear_s)

    gather_wait()

    def put(j, rows, val):
        hi = val.astype(BF16)
        X[j, 0, rows, :] = hi
        X[j, 1, rows, :] = (val - hi.astype(F32)).astype(BF16)

    def left(m, j):
        hi, lo = mat_ref[m], mat_ref[m + 1]
        xh, xl = X[j, 0], X[j, 1]
        return jnp.dot(jnp.concatenate([hi, lo, hi], 1), jnp.concatenate([xh, xh, xl], 0), preferred_element_type=F32)

    def right(j, m):
        hi, lo = mat_ref[m], mat_ref[m + 1]
        xh, xl = X[j, 0], X[j, 1]
        return jnp.dot(jnp.concatenate([xh, xl, xh], 1), jnp.concatenate([hi, hi, lo], 0), preferred_element_type=F32)

    step = 32

    def fold(val):
        return jnp.sum(val.reshape(-1, 8, val.shape[-1]), axis=0)

    def patch(s, acc):
        a = off_ref[2 * s] + h
        b = off_ref[2 * s + 1] + h
        ri = lax.broadcasted_iota(jnp.int32, (step, side), 0)
        in_col = lax.broadcasted_iota(jnp.int32, (step, side), 1) >= b
        for t in range(0, h, step):
            parts = []
            for base in (t, h + t):
                rows, far = slice(base, base + step), slice(side + base, side + base + step)
                in_row = ri + base >= a
                v = [
                    jnp.where(in_row, jnp.where(in_col, R[c, rows, 0:side], R[c, rows, side:]),
                              jnp.where(in_col, R[c, far, 0:side], R[c, far, side:]))
                    for c in range(2)
                ]
                p0, p1 = PR[s, 0, rows, :], PR[s, 1, rows, :]
                parts.append((p0 * v[0] - p1 * v[1], p0 * v[1] + p1 * v[0]))
            for c in range(2):
                rows = slice(c * h + t, c * h + t + step)
                put(0, rows, parts[0][c] + parts[1][c])
                put(1, rows, parts[0][c] - parts[1][c])
        Y[0] = left(0, 0)
        Y[1] = left(4, 1)
        for j in range(2):
            for t in range(0, h, step):
                re, im = Y[j, t:t + step, :], Y[j, h + t:h + t + step, :]
                rows = slice(j * h + t, j * h + t + step)
                put(2, rows, jnp.concatenate([re[:, :h] + re[:, h:], im[:, :h] + im[:, h:]], 1))
                put(3, rows, jnp.concatenate([re[:, :h] - re[:, h:], im[:, :h] - im[:, h:]], 1))
        Y[2] = right(2, 2)
        Y[3] = right(3, 6)
        for j in range(2):
            for t in range(0, side, step):
                rows = slice(t, t + step)
                f = Y[2 + j, rows, :]
                wf = W[j, rows, :] * f
                acc = acc + fold(wf * f)
                put(j, rows, wf)
        Y[0] = right(0, 0)
        Y[1] = right(1, 4)
        for j in range(2):
            for t in range(0, h, step):
                rows = slice(j * h + t, j * h + t + step)
                c, d = Y[0, rows, :], Y[1, rows, :]
                p, m = c + d, c - d
                put(2 + j, slice(t, t + step), jnp.concatenate([p[:, :h], m[:, :h]], 1))
                put(2 + j, slice(h + t, h + t + step), jnp.concatenate([p[:, h:], m[:, h:]], 1))
        Y[2] = left(2, 2)
        Y[3] = left(6, 3)
        for t in range(0, h, step):
            for sign, base in ((1, t), (-1, h + t)):
                rows, far = slice(base, base + step), slice(side + base, side + base + step)
                hr = Y[2, t:t + step, :] + sign * Y[3, t:t + step, :]
                hi = Y[2, h + t:h + t + step, :] + sign * Y[3, h + t:h + t + step, :]
                p0, p1 = PR[s, 0, rows, :], PR[s, 1, rows, :]
                in_row = ri + base >= a
                for c, term in ((0, p0 * hr + p1 * hi), (1, p0 * hi - p1 * hr)):
                    near_r = jnp.where(in_row, term, 0.0)
                    far_r = term - near_r
                    nn = jnp.where(in_col, near_r, 0.0)
                    fn = jnp.where(in_col, far_r, 0.0)
                    S[c, rows, 0:side] += nn
                    S[c, rows, side:] += near_r - nn
                    S[c, far, 0:side] += fn
                    S[c, far, side:] += far_r - fn
        return acc

    def copy_r(rows, _):
        R[:, rows, :] = G[:, rows, :]
    chunks(2 * side, 32, copy_r)

    ti = lax.broadcasted_iota(jnp.int32, (8, 128), 0)

    def lanes(acc):
        total = acc[:, 0:128]
        for q in range(128, acc.shape[1], 128):
            total = total + acc[:, q:q + 128]
        return jnp.sum(total, axis=0, keepdims=True)

    alpha = rr_before = None
    for it in range(ITERS):
        last = it + 1 == ITERS

        def norm(i, acc):
            v = R[:, pl.ds(pl.multiple_of(h + i * 32, 32), 32), own]
            return acc + fold(v[0] * v[0]) + fold(v[1] * v[1])
        rr_acc = lax.fori_loop(0, side // 32, norm, jnp.zeros((8, side), F32))
        acc = lax.fori_loop(0, cap, patch, jnp.zeros((8, side), F32))

        re_edge = [
            both(q, S.at[0, top_h, e], RA.at[0, :, e], S.at[0, end_h, e], RA.at[1, :, e], 0)
            for q, e in enumerate(edges)
        ]
        im_edge = [
            both(2 + q, S.at[1, e, top_h], CC.at[0, e, :], S.at[1, e, end_h], CC.at[1, e, :], 1)
            for q, e in enumerate(edges)
        ]
        re_mid = both(4, S.at[0, top_h, own], RA.at[0, :, own], S.at[0, end_h, own], RA.at[1, :, own], 0)
        im_mid = both(5, S.at[1, own, top_h], CC.at[0, own, :], S.at[1, own, end_h], CC.at[1, own, :], 1)
        for start, _ in (*re_edge, *im_edge, re_mid, im_mid):
            start()
        rr_l, pap_l = lanes(rr_acc), lanes(acc)
        T1[it, row] = jnp.where(ti == 0, rr_l, jnp.where(ti == 1, pap_l + RIDGE * rr_l, 0.0))
        ones = [
            pltpu.make_async_remote_copy(
                src_ref=T1.at[it, row], dst_ref=T1.at[it, row], send_sem=s1_send.at[it, d],
                recv_sem=s1_recv.at[it, d], device_id=(lax.rem(row + d, n_row), col), device_id_type=MESH)
            for d in range(1, n_row)
        ]
        for copy in ones:
            copy.start()
        for _, done in re_edge:
            done()

        def add_rows(i, carry):
            near = pl.ds(pl.multiple_of(i * 32, 32), 32)
            for q in range(2):
                rows = pl.ds(pl.multiple_of((1 + q) * h + i * 32, 32), 32)
                for e in edges:
                    S[0, rows, e] += RA[1 - q, near, e]
            return carry
        lax.fori_loop(0, h // 32, add_rows, 0)
        re_turn = both(6, S.at[0, own, top_h], CA.at[0], S.at[0, own, end_h], CA.at[1], 1)
        re_turn[0]()
        for _, done in im_edge:
            done()

        def add_cols(i, carry):
            for base in (0, 3 * h):
                rows = pl.ds(pl.multiple_of(base + i * 32, 32), 32)
                S[1, rows, one] += CC[1, rows, :]
                S[1, rows, two] += CC[0, rows, :]
            return carry
        lax.fori_loop(0, h // 32, add_cols, 0)
        im_turn = both(7, S.at[1, top_h, own], RC.at[0], S.at[1, end_h, own], RC.at[1], 0)
        im_turn[0]()
        for copy in ones:
            copy.wait()
        total = T1[it, 0]
        for q in range(1, n_row):
            total = total + T1[it, q]
        T2[it, col] = total
        twos = [
            pltpu.make_async_remote_copy(
                src_ref=T2.at[it, col], dst_ref=T2.at[it, col], send_sem=s2_send.at[it, d],
                recv_sem=s2_recv.at[it, d], device_id=(row, lax.rem(col + d, n_col)), device_id_type=MESH)
            for d in range(1, n_col)
        ]
        for copy in twos:
            copy.start()
        re_mid[1]()
        im_mid[1]()
        re_turn[1]()
        im_turn[1]()

        def make(i, carry):
            near = pl.ds(pl.multiple_of(i * 32, 32), 32)
            for q in range(2):
                rows = pl.ds(pl.multiple_of((1 + q) * h + i * 32, 32), 32)
                inner = pl.ds(pl.multiple_of(q * h + i * 32, 32), 32)
                re = S[0, rows, own] + RA[1 - q, near, own] + RIDGE * R[0, rows, own]
                im = S[1, rows, own] + RC[1 - q, near, :] + RIDGE * R[1, rows, own]
                G[0, rows, one] = re[:, :h] + CA[1, inner, :]
                G[0, rows, two] = re[:, h:] + CA[0, inner, :]
                G[1, rows, one] = im[:, :h] + CC[1, rows, :]
                G[1, rows, two] = im[:, h:] + CC[0, rows, :]
            return carry
        lax.fori_loop(0, h // 32, make, 0)
        gather_wait = None if last else gather()
        for copy in twos:
            copy.wait()
        total = T2[it, 0]
        for q in range(1, n_col):
            total = total + T2[it, q]
        rr = jnp.sum(jnp.where(ti == 0, total, 0.0), keepdims=True)
        pap = jnp.sum(jnp.where(ti == 1, total, 0.0), keepdims=True)
        if it == 0:
            ratio = None
            alpha = rr / pap
        else:
            ratio = rr / rr_before
            alpha = rr / (pap - ratio * rr / alpha)
        rr_before = rr

        def advance(i, carry):
            near = pl.ds(pl.multiple_of(i * 32, 32), 32)
            rows = pl.ds(pl.multiple_of(h + i * 32, 32), 32)
            for c in range(2):
                r = R[c, rows, own]
                d = r if it == 0 else r + ratio * D[c, near, :]
                if not last:
                    D[c, near, :] = d
                sol_ref[c, near, :] = alpha * d if it == 0 else sol_ref[c, near, :] + alpha * d
                if last:
                    along = G[c, rows, own] + ratio * L[c, rows, own]
                    res_ref[c, near, :] = r - alpha * along
            return carry
        lax.fori_loop(0, side // 32, advance, 0)
        if not last:
            chunks(2 * side, 32, clear_s)
            gather_wait()

            def advance_r(rows, _):
                for c in range(2):
                    along = G[c, rows, :] if it == 0 else G[c, rows, :] + ratio * L[c, rows, :]
                    L[c, rows, :] = along
                    R[c, rows, :] = R[c, rows, :] - alpha * along
            chunks(2 * side, 32, advance_r)


def solution(mesh):
    n_row, n_col = mesh.shape["row"], mesh.shape["col"]

    def local(right_side, probe, weights, offsets, counts):
        side = probe.shape[1]
        cap = offsets.shape[2]
        h = side // 2
        mats = jnp.asarray(tables(side))
        block = jax.ShapeDtypeStruct((2, side, side), F32)
        vmem = pl.BlockSpec(memory_space=pltpu.VMEM)
        smem = pl.BlockSpec(memory_space=pltpu.SMEM)
        wide = pltpu.VMEM((2, 2 * side, 2 * side), F32)
        dma = pltpu.SemaphoreType.DMA
        return pl.pallas_call(
            functools.partial(kernel, n_row, n_col, cap, side),
            out_shape=(block, block),
            in_specs=[smem, smem, vmem, vmem, vmem, vmem],
            out_specs=(vmem, vmem),
            scratch_shapes=[
                wide, wide, wide, wide,
                pltpu.VMEM((2, side, side), F32),
                pltpu.VMEM((cap, 2, side, side), F32),
                pltpu.VMEM((4, 2, side, side), BF16),
                pltpu.VMEM((4, side, side), F32),
                pltpu.VMEM((2, side, side), F32),
                pltpu.VMEM((2, h, 2 * side), F32),
                pltpu.VMEM((2, side, h), F32),
                pltpu.VMEM((2, 2 * side, h), F32),
                pltpu.VMEM((2, h, side), F32),
                pltpu.VMEM((ITERS, n_row, 8, 128), F32),
                pltpu.VMEM((ITERS, n_col, 8, 128), F32),
                dma((32,)), dma((32,)),
                dma((ITERS, n_row)), dma((ITERS, n_row)),
                dma((ITERS, n_col)), dma((ITERS, n_col)),
            ],
            compiler_params=pltpu.CompilerParams(
                collective_id=0, has_side_effects=True, vmem_limit_bytes=48 * 1024 * 1024),
        )(offsets.reshape(-1), counts.reshape(-1), right_side, probe, weights, mats)

    placed = (P(None, "row", "col"), P(), P(), P("row", "col", None, None), P("row", "col"))
    return jax.shard_map(
        local, mesh=mesh, in_specs=placed, out_specs=(P(None, "row", "col"), P(None, "row", "col")), check_vma=False)
```

profile of v0, /device:TPU:4, one launch (start us, length us, event | category | flops | bytes accessed | tf_op | source)
XLA Modules:
  0.0 100.6 jit_solution(8768271720397954846)
XLA Ops:
  1.3 0.0 copy-start.4
  1.3 0.7 copy-done.4
  2.0 0.1 copy.9
  2.0 0.1 reshape.10.off_ref
  2.1 0.0 copy-start
  2.1 1.2 %copy-done = bf16[8,256,256]{2,1,0:T(8,128)(2,1)S(1)} copy-done((bf16[8,256,256]{2,1,0:T(8,128)(2,1)S(1)}, bf16[8,256,256]{2,1,0:T(8,128)(2,1)}, u32[]{:S(2)}) %copy-start) | copy-done | bytes 1048600
  3.4 0.0 copy-start.1
  3.4 1.0 %copy-done.1 = f32[2,256,256]{2,1,0:T(8,128)S(1)} copy-done((f32[2,256,256]{2,1,0:T(8,128)S(1)}, f32[2,256,256]{2,1,0:T(8,128)}, u32[]{:S(2)}) %copy-start.1) | copy-done | bytes 524312
  4.4 0.0 copy-start.2
  4.4 1.0 %copy-done.2 = f32[2,256,256]{2,1,0:T(8,128)S(1)} copy-done((f32[2,256,256]{2,1,0:T(8,128)S(1)}, f32[2,256,256]{2,1,0:T(8,128)}, u32[]{:S(2)}) %copy-start.2) | copy-done | bytes 524312
  5.4 0.0 copy-start.3
  5.4 0.9 copy-done.3
  6.4 92.6 %shard_map.77 = (f32[2,256,256]{2,1,0:T(8,128)S(1)}, f32[2,256,256]{2,1,0:T(8,128)S(1)}) custom-call(s32[8]{0:T(128)S(1)} %reshape.10.off_ref, s32[1]{0:T(128)} %bitcast.1.cnt_ref, f32[2,256,256]{2,1,0:T(8,128)S(1)} %copy-done.1, f32[2,256,256]{2,1,0:T(8,128)S(1)} %copy-done.2, f32[256,256]{1,0:T(8,128)S(1)} %copy-done.3, bf16[8,256,256]{2,1,0:T(8,128)(2,1)S(1)} %copy-done), custom_call_target="tpu_custom_call" | custom-call | tf_op jit(solution)/shard_map/pallas_call | solution.py:400
  99.0 0.8 copy.13
  99.8 0.8 copy.14
Async XLA Ops:
  1.3 0.7 copy-start.4
  2.1 1.2 %copy-start = (bf16[8,256,256]{2,1,0:T(8,128)(2,1)S(1)}, bf16[8,256,256]{2,1,0:T(8,128)(2,1)}, u32[]{:S(2)}) copy-start(bf16[8,256,256]{2,1,0:T(8,128)(2,1)} %constant.2.clone.mat_ref) | copy-start | bytes 3145732
  3.4 1.0 %copy-start.1 = (f32[2,256,256]{2,1,0:T(8,128)S(1)}, f32[2,256,256]{2,1,0:T(8,128)}, u32[]{:S(2)}) copy-start(f32[2,256,256]{2,1,0:T(8,128)} %rhs_ref.1) | copy-start | bytes 1572868
  4.4 1.0 %copy-start.2 = (f32[2,256,256]{2,1,0:T(8,128)S(1)}, f32[2,256,256]{2,1,0:T(8,128)}, u32[]{:S(2)}) copy-start(f32[2,256,256]{2,1,0:T(8,128)} %probe_ref.1) | copy-start | bytes 1572868
  5.4 0.9 copy-start.3
where the time goes:
time: 103 us; the launch traced here: 101 us
  Pallas kernels  92.6 us (90%)
  local copies, waits for them, and re-layouts  6.7 us (7%)
  between operations  1.3 us (1%)
    pallas_call x1, Pallas kernels, local(): pl.pallas_call(functools.partial(kernel, n_row, n_col, cap, side), out_sh...  92.6 us
    unnamed x13, local copies, waits for them, and re-layouts  6.61 us

commit v1 on v0

v1 whole, which is shorter than its diff:
```python
import functools
import math

import jax
import jax.numpy as jnp
import numpy as np
from jax import lax
from jax.experimental import pallas as pl
from jax.experimental.pallas import tpu as pltpu
from jax.sharding import PartitionSpec as P

ITERS = 3
RIDGE = 0.5
SKEW = 4.5
MESH = pl.DeviceIdType.MESH
F32 = jnp.float32
BF16 = jnp.bfloat16


def tables(length):
    half = length // 2
    k = np.arange(half)[:, None]
    n = np.arange(half)[None, :]
    out = []
    for odd in (0, 1):
        angle = 2.0 * math.pi * ((n * (2 * k + odd)) % length) / length
        re, im = np.cos(angle) / math.sqrt(length), -np.sin(angle) / math.sqrt(length)
        real = np.block([[re, -im], [im, re]])
        for mat in (real, real.T):
            hi = mat.astype(BF16)
            out += [hi, (mat - hi.astype(np.float64)).astype(BF16)]
    return np.stack(out)


def kernel(
    n_row, n_col, cap, side,
    off_ref, cnt_ref, rhs_hbm, probe_hbm, w_hbm, mat_hbm,
    SOL, res_ref,
    R, G, L, S, D, PR, P0, W0, mat_ref, XA, XB, YA, YB, W, RA, CA, CC, RC, T1, T2,
    bar_send, bar_recv, s1_send, s1_recv, s2_send, s2_recv, io_sem,
):
    h = side // 2
    own = slice(h, h + side)
    row = lax.axis_index("row")
    col = lax.axis_index("col")

    load_r = pltpu.make_async_copy(rhs_hbm, R.at[:, own, own], io_sem.at[0])
    load_p = pltpu.make_async_copy(probe_hbm, P0, io_sem.at[1])
    load_w = pltpu.make_async_copy(w_hbm, W0, io_sem.at[2])
    load_m = pltpu.make_async_copy(mat_hbm, mat_ref, io_sem.at[3])
    for load in (load_r, load_p, load_w, load_m):
        load.start()

    def chunks(total, step, body):
        def run(i, carry):
            body(pl.ds(pl.multiple_of(i * step, step), step))
            return carry
        lax.fori_loop(0, total // step, run, 0)

    def fill(buf, rows, cols):
        def run(i, carry):
            at = pl.ds(pl.multiple_of(rows.start + i * 32, 32), 32)
            buf[:, at, cols] = jnp.zeros((2, 32, cols.stop - cols.start), F32)
            return carry
        lax.fori_loop(0, (rows.stop - rows.start) // 32, run, 0)

    every = slice(0, 2 * side)
    for rows in (slice(0, h), slice(3 * h, 4 * h)):
        fill(R, rows, every)
    for cols in (slice(0, h), slice(3 * h, 4 * h)):
        fill(R, own, cols)
    for buf in (RA, CA, CC, RC):
        fill(buf, slice(0, buf.shape[1]), slice(0, buf.shape[2]))
    barrier = pltpu.get_barrier_semaphore()
    for d in range(1, n_row):
        pl.semaphore_signal(barrier, inc=1, device_id=(lax.rem(row + d, n_row), col), device_id_type=MESH)
    for d in range(1, n_col):
        pl.semaphore_signal(barrier, inc=1, device_id=(row, lax.rem(col + d, n_col)), device_id_type=MESH)
    pl.semaphore_wait(barrier, n_row - 1 + n_col - 1)

    def both(index, low_src, low_dst, high_src, high_dst, axis):
        at, count = (row, n_row) if axis == 0 else (col, n_col)

        def target(step):
            return (row + step, col) if axis == 0 else (row, col + step)

        low = pltpu.make_async_remote_copy(
            src_ref=low_src, dst_ref=low_dst, send_sem=bar_send.at[2 * index], recv_sem=bar_recv.at[2 * index],
            device_id=target(-1), device_id_type=MESH)
        high = pltpu.make_async_remote_copy(
            src_ref=high_src, dst_ref=high_dst, send_sem=bar_send.at[2 * index + 1],
            recv_sem=bar_recv.at[2 * index + 1], device_id=target(1), device_id_type=MESH)

        def start():
            pl.when(at > 0)(low.start)
            pl.when(at < count - 1)(high.start)

        def wait():
            @pl.when(at > 0)
            def _():
                low.wait_send()
                high.wait_recv()

            @pl.when(at < count - 1)
            def _():
                high.wait_send()
                low.wait_recv()

        return start, wait

    edges = (slice(0, h), slice(3 * h, 4 * h))
    one, two, top_h, end_h = slice(h, 2 * h), slice(2 * h, 3 * h), slice(0, h), slice(3 * h, 4 * h)

    def gather(F):
        re_turn = both(8, F.at[0, own, one], F.at[0, own, end_h], F.at[0, own, two], F.at[0, own, top_h], 1)
        im_turn = both(9, F.at[1, one, own], F.at[1, end_h, own], F.at[1, two, own], F.at[1, top_h, own], 0)
        rest = [
            both(10, F.at[0, one, own], F.at[0, end_h, own], F.at[0, two, own], F.at[0, top_h, own], 0),
            both(11, F.at[1, own, one], F.at[1, own, end_h], F.at[1, own, two], F.at[1, own, top_h], 1),
        ]
        for start, _ in (re_turn, im_turn, *rest):
            start()
        re_turn[1]()
        for q, e in enumerate(edges):
            rest.append(both(12 + q, F.at[0, one, e], F.at[0, end_h, e], F.at[0, two, e], F.at[0, top_h, e], 0))
            rest[-1][0]()
        im_turn[1]()
        for q, e in enumerate(edges):
            rest.append(both(14 + q, F.at[1, e, one], F.at[1, e, end_h], F.at[1, e, two], F.at[1, e, top_h], 1))
            rest[-1][0]()

        def wait():
            for _, done in rest:
                done()

        return wait

    load_r.wait()
    gather_wait = gather(R)

    fill(G, every, every)
    fill(L, every, every)
    for buf in (D, SOL):
        fill(buf, slice(0, buf.shape[1]), slice(0, buf.shape[2]))

    load_p.wait()
    for s in range(cap):
        on = jnp.where(s < cnt_ref[0, 0], 1.0, 0.0).astype(F32)
        for c in range(2):
            rolled = pltpu.roll(P0[c], off_ref[0, s] + h, 0)
            PR[s, c] = pltpu.roll(rolled, off_ref[1, s] + h, 1) * on

    def three(val):
        top = val.astype(BF16)
        rest = val - top.astype(F32)
        mid = rest.astype(BF16)
        return top, mid, (rest - mid.astype(F32)).astype(BF16)

    load_w.wait()
    first = lax.broadcasted_iota(jnp.int32, (side, side), 0)
    second = lax.broadcasted_iota(jnp.int32, (side, side), 1)
    freq = jnp.where(first >= h, 2 * (first - h) + 1, 2 * first)
    pick = jnp.where(second == freq, 1.0, 0.0).astype(BF16)
    by_row = sum(jnp.dot(pick, part, preferred_element_type=F32) for part in three(W0[...]))
    parts = three(by_row)
    lane = jnp.where(second >= h, second - h, second)
    for q in range(2):
        pick = jnp.where(first == 2 * lane + q, 1.0, 0.0).astype(BF16)
        W[q] = sum(jnp.dot(part, pick, preferred_element_type=F32) for part in parts)

    load_m.wait()
    gather_wait()

    step = 32

    def fold(val):
        return jnp.sum(val.reshape(-1, 8, val.shape[-1]), axis=0)

    sub = lax.broadcasted_iota(jnp.int32, (step, h), 0)
    lan = lax.broadcasted_iota(jnp.int32, (step, h), 1)

    def side_of(s, at):
        if s == 0:
            return "both" if at < h else "near"
        if s == 1:
            return "far" if at < h else "both"
        return "both"

    def patch(s, k, seen, acc):
        X, Y = (XA, YA) if k == 0 else (XB, YB)
        a = off_ref[0, s] + h
        b = off_ref[1, s] + h

        def put(j, rows, val):
            hi = val.astype(BF16)
            X[j, 0, rows, :] = hi
            X[j, 1, rows, :] = (val - hi.astype(F32)).astype(BF16)

        def left(m, j):
            hi, lo = mat_ref[m], mat_ref[m + 1]
            xh, xl = X[j, 0], X[j, 1]
            return jnp.dot(
                jnp.concatenate([hi, lo, hi], 1), jnp.concatenate([xh, xh, xl], 0), preferred_element_type=F32)

        def right(j, m):
            hi, lo = mat_ref[m], mat_ref[m + 1]
            xh, xl = X[j, 0], X[j, 1]
            return jnp.dot(
                jnp.concatenate([xh, xl, xh], 1), jnp.concatenate([hi, hi, lo], 0), preferred_element_type=F32)

        def covered(c, base):
            halves = []
            for at in (0, h):
                cols, fcols = slice(at, at + h), slice(side + at, side + at + h)
                rk, ck = side_of(s, base), side_of(s, at)
                rows, far = slice(base, base + step), slice(side + base, side + base + step)

                def in_cols(r):
                    if ck == "near":
                        return R[c, r, cols]
                    if ck == "far":
                        return R[c, r, fcols]
                    return jnp.where(lan + at >= b, R[c, r, cols], R[c, r, fcols])

                if rk == "near":
                    halves.append(in_cols(rows))
                elif rk == "far":
                    halves.append(in_cols(far))
                else:
                    halves.append(jnp.where(sub + base >= a, in_cols(rows), in_cols(far)))
            return jnp.concatenate(halves, 1)

        def scatter(c, base, term):
            for at in (0, h):
                val = term[:, at:at + h]
                rk, ck = side_of(s, base), side_of(s, at)
                rows = {}
                if rk == "both":
                    near = jnp.where(sub + base >= a, val, 0.0)
                    rows = {0: near, side: val - near}
                else:
                    rows = {0 if rk == "near" else side: val}
                for shift, part in rows.items():
                    if ck == "both":
                        near = jnp.where(lan + at >= b, part, 0.0)
                        cells = {0: near, side: part - near}
                    else:
                        cells = {0 if ck == "near" else side: part}
                    for over, cell in cells.items():
                        r0, c0 = shift + base, over + at
                        where = (c, slice(r0, r0 + step), slice(c0, c0 + h))
                        if (c, r0, c0) in seen:
                            S[where] += cell
                        else:
                            S[where] = cell
                            seen.add((c, r0, c0))

        def load():
            for t in range(0, h, step):
                parts = []
                for base in (t, h + t):
                    rows = slice(base, base + step)
                    v = [covered(c, base) for c in range(2)]
                    p0, p1 = PR[s, 0, rows, :], PR[s, 1, rows, :]
                    parts.append((p0 * v[0] - p1 * v[1], p0 * v[1] + p1 * v[0]))
                for c in range(2):
                    rows = slice(c * h + t, c * h + t + step)
                    put(0, rows, parts[0][c] + parts[1][c])
                    put(1, rows, parts[0][c] - parts[1][c])

        def mul_a():
            Y[0] = left(0, 0)
            Y[1] = left(4, 1)

        def mix_b():
            for j in range(2):
                for t in range(0, h, step):
                    re, im = Y[j, t:t + step, :], Y[j, h + t:h + t + step, :]
                    rows = slice(j * h + t, j * h + t + step)
                    put(2, rows, jnp.concatenate([re[:, :h] + re[:, h:], im[:, :h] + im[:, h:]], 1))
                    put(3, rows, jnp.concatenate([re[:, :h] - re[:, h:], im[:, :h] - im[:, h:]], 1))

        def mul_b():
            Y[2] = right(2, 2)
            Y[3] = right(3, 6)

        def mix_c():
            for j in range(2):
                for t in range(0, side, step):
                    rows = slice(t, t + step)
                    f = Y[2 + j, rows, :]
                    wf = W[j, rows, :] * f
                    acc[0] = acc[0] + fold(wf * f)
                    put(j, rows, wf)

        def mul_c():
            Y[0] = right(0, 0)
            Y[1] = right(1, 4)

        def mix_d():
            for j in range(2):
                for t in range(0, h, step):
                    rows = slice(j * h + t, j * h + t + step)
                    c, d = Y[0, rows, :], Y[1, rows, :]
                    p, m = c + d, c - d
                    put(2 + j, slice(t, t + step), jnp.concatenate([p[:, :h], m[:, :h]], 1))
                    put(2 + j, slice(h + t, h + t + step), jnp.concatenate([p[:, h:], m[:, h:]], 1))

        def mul_d():
            Y[2] = left(2, 2)
            Y[3] = left(6, 3)

        def store():
            for t in range(0, h, step):
                for sign, base in ((1, t), (-1, h + t)):
                    rows = slice(base, base + step)
                    if sign == 1:
                        hr = Y[2, t:t + step, :] + Y[3, t:t + step, :]
                        hi = Y[2, h + t:h + t + step, :] + Y[3, h + t:h + t + step, :]
                    else:
                        hr = Y[2, t:t + step, :] - Y[3, t:t + step, :]
                        hi = Y[2, h + t:h + t + step, :] - Y[3, h + t:h + t + step, :]
                    p0, p1 = PR[s, 0, rows, :], PR[s, 1, rows, :]
                    scatter(0, base, p0 * hr + p1 * hi)
                    scatter(1, base, p0 * hi - p1 * hr)

        return [load, mul_a, mix_b, mul_b, mix_c, mul_c, mix_d, mul_d, store]

    ti = lax.broadcasted_iota(jnp.int32, (8, 128), 0)

    def lanes(acc):
        total = acc[:, 0:128]
        for q in range(128, acc.shape[1], 128):
            total = total + acc[:, q:q + 128]
        return jnp.sum(total, axis=0, keepdims=True)

    def iteration(it, carry):
        alpha_before, rr_before = carry
        last = it + 1 == ITERS

        def norm(i, acc):
            v = R[:, pl.ds(pl.multiple_of(h + i * 32, 32), 32), own]
            return acc + fold(v[0] * v[0]) + fold(v[1] * v[1])
        rr_acc = lax.fori_loop(0, side // 32, norm, jnp.zeros((8, side), F32))

        order = [*range(2, cap), 0, 1]
        seen = set()
        acc = [jnp.zeros((8, side), F32)]
        timed = []
        for n, s in enumerate(order):
            for q, stage in enumerate(patch(s, n % 2, seen, acc)):
                timed.append((SKEW * n + q, n, stage))
        for _, _, stage in sorted(timed, key=lambda x: x[:2]):
            stage()
        acc = acc[0]

        re_edge = [
            both(q, S.at[0, top_h, e], RA.at[0, :, e], S.at[0, end_h, e], RA.at[1, :, e], 0)
            for q, e in enumerate(edges)
        ]
        im_edge = [
            both(2 + q, S.at[1, e, top_h], CC.at[0, e, :], S.at[1, e, end_h], CC.at[1, e, :], 1)
            for q, e in enumerate(edges)
        ]
        re_mid = both(4, S.at[0, top_h, own], RA.at[0, :, own], S.at[0, end_h, own], RA.at[1, :, own], 0)
        im_mid = both(5, S.at[1, own, top_h], CC.at[0, own, :], S.at[1, own, end_h], CC.at[1, own, :], 1)
        for start, _ in (*re_edge, *im_edge, re_mid, im_mid):
            start()
        rr_l, pap_l = lanes(rr_acc), lanes(acc)
        T1[it, row] = jnp.where(ti == 0, rr_l, jnp.where(ti == 1, pap_l + RIDGE * rr_l, 0.0))
        ones = [
            pltpu.make_async_remote_copy(
                src_ref=T1.at[it, row], dst_ref=T1.at[it, row], send_sem=s1_send.at[it, d],
                recv_sem=s1_recv.at[it, d], device_id=(lax.rem(row + d, n_row), col), device_id_type=MESH)
            for d in range(1, n_row)
        ]
        for copy in ones:
            copy.start()
        for _, done in re_edge:
            done()

        def add_rows(i, carry):
            near = pl.ds(pl.multiple_of(i * 32, 32), 32)
            for q in range(2):
                rows = pl.ds(pl.multiple_of((1 + q) * h + i * 32, 32), 32)
                for e in edges:
                    S[0, rows, e] += RA[1 - q, near, e]
            return carry
        lax.fori_loop(0, h // 32, add_rows, 0)
        re_turn = both(6, S.at[0, own, top_h], CA.at[0], S.at[0, own, end_h], CA.at[1], 1)
        re_turn[0]()
        for _, done in im_edge:
            done()

        def add_cols(i, carry):
            for base in (0, 3 * h):
                rows = pl.ds(pl.multiple_of(base + i * 32, 32), 32)
                S[1, rows, one] += CC[1, rows, :]
                S[1, rows, two] += CC[0, rows, :]
            return carry
        lax.fori_loop(0, h // 32, add_cols, 0)
        im_turn = both(7, S.at[1, top_h, own], RC.at[0], S.at[1, end_h, own], RC.at[1], 0)
        im_turn[0]()
        for copy in ones:
            copy.wait()
        total = T1[it, 0]
        for q in range(1, n_row):
            total = total + T1[it, q]
        T2[it, col] = total
        twos = [
            pltpu.make_async_remote_copy(
                src_ref=T2.at[it, col], dst_ref=T2.at[it, col], send_sem=s2_send.at[it, d],
                recv_sem=s2_recv.at[it, d], device_id=(row, lax.rem(col + d, n_col)), device_id_type=MESH)
            for d in range(1, n_col)
        ]
        for copy in twos:
            copy.start()
        re_mid[1]()
        im_mid[1]()
        re_turn[1]()
        im_turn[1]()

        def make(i, carry):
            near = pl.ds(pl.multiple_of(i * 32, 32), 32)
            for q in range(2):
                rows = pl.ds(pl.multiple_of((1 + q) * h + i * 32, 32), 32)
                inner = pl.ds(pl.multiple_of(q * h + i * 32, 32), 32)
                re = S[0, rows, own] + RA[1 - q, near, own]
                im = S[1, rows, own] + RC[1 - q, near, :]
                G[0, rows, one] = re[:, :h] + CA[1, inner, :]
                G[0, rows, two] = re[:, h:] + CA[0, inner, :]
                G[1, rows, one] = im[:, :h] + CC[1, rows, :]
                G[1, rows, two] = im[:, h:] + CC[0, rows, :]
            return carry
        lax.fori_loop(0, h // 32, make, 0)

        def scalars():
            for copy in twos:
                copy.wait()
            total = T2[it, 0]
            for q in range(1, n_col):
                total = total + T2[it, q]
            rr = jnp.sum(jnp.where(ti == 0, total, 0.0), keepdims=True)
            pap = jnp.sum(jnp.where(ti == 1, total, 0.0), keepdims=True)
            ratio = jnp.where(it == 0, 0.0, rr / rr_before)
            return rr, ratio, rr / (pap - ratio * rr / alpha_before)

        @pl.when(jnp.logical_not(last))
        def _():
            wait = gather(G)
            wait()

        rr, ratio, alpha = scalars()

        def advance(i, carry):
            near = pl.ds(pl.multiple_of(i * 32, 32), 32)
            rows = pl.ds(pl.multiple_of(h + i * 32, 32), 32)
            for c in range(2):
                d = R[c, rows, own] + ratio * D[c, near, :]
                D[c, near, :] = d
                SOL[c, near, :] += alpha * d
            return carry
        lax.fori_loop(0, side // 32, advance, 0)

        def advance_r(rows):
            for c in range(2):
                r = R[c, rows, :]
                along = G[c, rows, :] + RIDGE * r + ratio * L[c, rows, :]
                L[c, rows, :] = along
                R[c, rows, :] = r - alpha * along
        chunks(2 * side, 32, advance_r)
        return alpha, rr

    one11 = jnp.ones((1, 1), F32)
    lax.fori_loop(0, ITERS, iteration, (one11, one11))

    def emit(rows):
        res_ref[:, rows, :] = R[:, pl.ds(pl.multiple_of(rows.start + h, 32), 32), own]
    chunks(side, 32, emit)


def solution(mesh):
    n_row, n_col = mesh.shape["row"], mesh.shape["col"]

    def local(right_side, probe, weights, offsets, counts):
        side = probe.shape[1]
        cap = offsets.shape[2]
        h = side // 2
        mats = jnp.asarray(tables(side))
        block = jax.ShapeDtypeStruct((2, side, side), F32)
        hbm = pl.BlockSpec(memory_space=pltpu.HBM)
        smem = pl.BlockSpec(memory_space=pltpu.SMEM)
        wide = pltpu.VMEM((2, 2 * side, 2 * side), F32)
        tile = pltpu.VMEM((2, side, side), F32)
        dma = pltpu.SemaphoreType.DMA
        vmem = pl.BlockSpec(memory_space=pltpu.VMEM)
        return pl.pallas_call(
            functools.partial(kernel, n_row, n_col, cap, side),
            out_shape=(block, block),
            in_specs=[smem, smem, hbm, hbm, hbm, hbm],
            out_specs=(vmem, vmem),
            scratch_shapes=[
                wide, wide, wide, wide,
                tile,
                pltpu.VMEM((cap, 2, side, side), F32),
                tile,
                pltpu.VMEM((side, side), F32),
                pltpu.VMEM((8, side, side), BF16),
                pltpu.VMEM((4, 2, side, side), BF16),
                pltpu.VMEM((4, 2, side, side), BF16),
                pltpu.VMEM((4, side, side), F32),
                pltpu.VMEM((4, side, side), F32),
                tile,
                pltpu.VMEM((2, h, 2 * side), F32),
                pltpu.VMEM((2, side, h), F32),
                pltpu.VMEM((2, 2 * side, h), F32),
                pltpu.VMEM((2, h, side), F32),
                pltpu.VMEM((ITERS, n_row, 8, 128), F32),
                pltpu.VMEM((ITERS, n_col, 8, 128), F32),
                dma((32,)), dma((32,)),
                dma((ITERS, n_row)), dma((ITERS, n_row)),
                dma((ITERS, n_col)), dma((ITERS, n_col)),
                dma((4,)),
            ],
            compiler_params=pltpu.CompilerParams(
                collective_id=0, has_side_effects=True, vmem_limit_bytes=53824 * 1024),
        )(offsets[0, 0].T, counts, right_side, probe, weights, mats)

    placed = (P(None, "row", "col"), P(), P(), P("row", "col", None, None), P("row", "col"))
    return jax.shard_map(
        local, mesh=mesh, in_specs=placed, out_specs=(P(None, "row", "col"), P(None, "row", "col")), check_vma=False)
```

time: 103 us -> 93.9 us (0.912)
  Pallas kernels: 92.6 us -> 87.5 us
  local copies, waits for them, and re-layouts: 6.7 us -> 3.21 us
    pallas_call x1, Pallas kernels: 92.6 us -> 87.5 us  [local(): pl.pallas_call(functools.partial(kernel, n_row, n_col, cap, side), out_sh...]
    unnamed x13 -> x6, local copies, waits for them, and re-layouts: 6.61 us -> 3.21 us
where the time goes in v1:
time: 93.9 us; the launch traced here: 92 us
  Pallas kernels  87.5 us (93%)
  local copies, waits for them, and re-layouts  3.21 us (3%)
  between operations  1.3 us (1%)
    pallas_call x1, Pallas kernels, local(): pl.pallas_call(functools.partial(kernel, n_row, n_col, cap, side), out_sh...  87.5 us
    unnamed x6, local copies, waits for them, and re-layouts  3.21 us

profile of v1, /device:TPU:4, one launch (start us, length us, event | category | flops | bytes accessed | tf_op | source)
XLA Modules:
  0.0 92.0 jit_solution(17835440968580371606)
XLA Ops:
  1.3 0.0 copy-start.1
  1.3 0.7 copy-done.1
  2.0 0.0 copy-start
  2.0 0.9 %copy-done = f32[256,256]{1,0:T(8,128)S(1)} copy-done((f32[256,256]{1,0:T(8,128)S(1)}, f32[256,256]{1,0:T(8,128)}, u32[]{:S(2)}) %copy-start) | copy-done | bytes 262168
  2.9 87.5 %shard_map.77 = (f32[2,256,256]{2,1,0:T(8,128)S(1)}, f32[2,256,256]{2,1,0:T(8,128)S(1)}) custom-call(s32[2,4]{1,0:T(2,128)S(1)} %bitcast.3, s32[1,1]{1,0:T(1,128)S(6)} %copy.10.cnt_ref, f32[2,256,256]{2,1,0:T(8,128)} %rhs_hbm.1, f32[2,256,256]{2,1,0:T(8,128)} %probe_hbm.1, f32[256,256]{1,0:T(8,128)S(1)} %copy-done, bf16[8,256,256]{2,1,0:T(8,128)(2,1)} %constant.2.clone.mat_hbm), custom_call_target="tpu_custom_call" | custom-call | tf_op jit(solution)/shard_map/pallas_call | solution.py:497
  90.4 0.8 copy.11
  91.2 0.8 copy.12
Async XLA Ops:
  1.3 0.7 copy-start.1
  2.0 0.9 %copy-start = (f32[256,256]{1,0:T(8,128)S(1)}, f32[256,256]{1,0:T(8,128)}, u32[]{:S(2)}) copy-start(f32[256,256]{1,0:T(8,128)} %w_hbm.1) | copy-start | bytes 786436

commit v2 on v1

--- a/solution.py
+++ b/solution.py
@@ -11,7 +11,7 @@
 
 ITERS = 3
 RIDGE = 0.5
-SKEW = 4.5
+SKEW = 1.0
 MESH = pl.DeviceIdType.MESH
 F32 = jnp.float32
 BF16 = jnp.bfloat16
@@ -33,11 +33,11 @@
 
 
 def kernel(
-    n_row, n_col, cap, side,
+    n_row, n_col, n_x, cap, side,
     off_ref, cnt_ref, rhs_hbm, probe_hbm, w_hbm, mat_hbm,
     SOL, res_ref,
-    R, G, L, S, D, PR, P0, W0, mat_ref, XA, XB, YA, YB, W, RA, CA, CC, RC, T1, T2,
-    bar_send, bar_recv, s1_send, s1_recv, s2_send, s2_recv, io_sem,
+    R, G, L, S, D, PR, P0, W0, mat_ref, XS, YS, W, RXI, RXO, DXI, DXO, ZR, DZ, T1, T2,
+    one_send, one_recv, two_send, two_recv, s1_send, s1_recv, s2_send, s2_recv, io_sem,
 ):
     h = side // 2
     own = slice(h, h + side)
@@ -53,24 +53,25 @@
 
     def chunks(total, step, body):
         def run(i, carry):
-            body(pl.ds(pl.multiple_of(i * step, step), step))
+            body(pl.multiple_of(i * step, step))
             return carry
         lax.fori_loop(0, total // step, run, 0)
 
     def fill(buf, rows, cols):
-        def run(i, carry):
-            at = pl.ds(pl.multiple_of(rows.start + i * 32, 32), 32)
-            buf[:, at, cols] = jnp.zeros((2, 32, cols.stop - cols.start), F32)
-            return carry
-        lax.fori_loop(0, (rows.stop - rows.start) // 32, run, 0)
+        def run(at):
+            buf[:, pl.ds(pl.multiple_of(rows.start + at, 32), 32), cols] = jnp.zeros(
+                (2, 32, cols.stop - cols.start), F32)
+        chunks(rows.stop - rows.start, 32, run)
 
     every = slice(0, 2 * side)
-    for rows in (slice(0, h), slice(3 * h, 4 * h)):
-        fill(R, rows, every)
-    for cols in (slice(0, h), slice(3 * h, 4 * h)):
-        fill(R, own, cols)
-    for buf in (RA, CA, CC, RC):
-        fill(buf, slice(0, buf.shape[1]), slice(0, buf.shape[2]))
+    one, two, top_h, end_h = slice(h, 2 * h), slice(2 * h, 3 * h), slice(0, h), slice(3 * h, 4 * h)
+    lefts, rights = slice(0, side), slice(side, 2 * side)
+    left_ok, right_ok = col > 0, col < n_col - 1
+    pl.when(row == 0)(lambda: fill(R, top_h, every))
+    pl.when(row == n_row - 1)(lambda: fill(R, end_h, every))
+    pl.when(col == 0)(lambda: fill(R, every, top_h))
+    pl.when(col == n_col - 1)(lambda: fill(R, every, end_h))
+
     barrier = pltpu.get_barrier_semaphore()
     for d in range(1, n_row):
         pl.semaphore_signal(barrier, inc=1, device_id=(lax.rem(row + d, n_row), col), device_id_type=MESH)
@@ -78,65 +79,95 @@
         pl.semaphore_signal(barrier, inc=1, device_id=(row, lax.rem(col + d, n_col)), device_id_type=MESH)
     pl.semaphore_wait(barrier, n_row - 1 + n_col - 1)
 
-    def both(index, low_src, low_dst, high_src, high_dst, axis):
-        at, count = (row, n_row) if axis == 0 else (col, n_col)
-
-        def target(step):
-            return (row + step, col) if axis == 0 else (row, col + step)
-
-        low = pltpu.make_async_remote_copy(
-            src_ref=low_src, dst_ref=low_dst, send_sem=bar_send.at[2 * index], recv_sem=bar_recv.at[2 * index],
-            device_id=target(-1), device_id_type=MESH)
-        high = pltpu.make_async_remote_copy(
-            src_ref=high_src, dst_ref=high_dst, send_sem=bar_send.at[2 * index + 1],
-            recv_sem=bar_recv.at[2 * index + 1], device_id=target(1), device_id_type=MESH)
-
-        def start():
-            pl.when(at > 0)(low.start)
-            pl.when(at < count - 1)(high.start)
+    odd = lax.rem(row, 2)
+    inner_row = row + 1 - 2 * odd
+    outer_row = row - 1 + 2 * odd
+    inner_ok = inner_row < n_row
+    outer_ok = jnp.logical_and(outer_row >= 0, outer_row < n_row)
+    bent = lax.rem((row + 1) // 2, n_x) == 0
+    z_first = (jnp.logical_and(bent, outer_ok), outer_ok)
+    x_first = tuple(jnp.logical_not(z) for z in z_first)
+    x_pair = tuple(jnp.logical_and(x, outer_ok) for x in x_first)
+
+    def band(start, size=h):
+        return pl.ds(pl.multiple_of(start, h), size)
+
+    inn, inn_halo, inn_there = band((2 - odd) * h), band(3 * h * (1 - odd)), band(3 * h * odd)
+    out, out_halo, out_there = band((1 + odd) * h), band(3 * h * odd), band(3 * h * (1 - odd))
+    outer = band(2 * h * odd, side)
+
+    class Swap:
+        def __init__(self, sems, parts):
+            send, recv = sems
+            self.parts = []
+            for q, (src, dst, device, sends, gets) in enumerate(parts):
+                self.parts.append((pltpu.make_async_remote_copy(
+                    src_ref=src, dst_ref=dst, send_sem=send(q), recv_sem=recv(q),
+                    device_id=device, device_id_type=MESH), sends, gets))
+
+        def start(self):
+            for copy, sends, _ in self.parts:
+                pl.when(sends)(copy.start)
+
+        def wait(self):
+            for copy, sends, gets in self.parts:
+                pl.when(sends)(copy.wait_send)
+                pl.when(gets)(copy.wait_recv)
+
+    def once(index):
+        return (lambda q: one_send.at[index + q]), (lambda q: one_recv.at[index + q])
+
+    def turn(index, phase):
+        return (lambda q: two_send.at[phase, index + q]), (lambda q: two_recv.at[phase, index + q])
+
+    def across(sems, left_src, left_dst, right_src, right_dst, on):
+        go_left, go_right = jnp.logical_and(on, left_ok), jnp.logical_and(on, right_ok)
+        return Swap(sems, [
+            (left_src, left_dst, (row, col - 1), go_left, go_right),
+            (right_src, right_dst, (row, col + 1), go_right, go_left)])
+
+    def along(sems, src, dst, there, on):
+        return Swap(sems, [(src, dst, (there, col), on, on)])
+
+    yes = col >= 0
+
+    def spread(F):
+        ends = [
+            across(once(20 + 2 * c), F.at[c, out, one], F.at[c, out, end_h], F.at[c, out, two], F.at[c, out, top_h], yes)
+            for c in range(2)
+        ]
+        mids = across(once(24), F.at[:, inn, one], F.at[:, inn, end_h], F.at[:, inn, two], F.at[:, inn, top_h], yes)
+        firsts = [along(once(26 + c), F.at[c, out, own], F.at[c, out_there, own], outer_row, z_first[c]) for c in range(2)]
+        ends[0].start()
+        firsts[1].start()
+        firsts[0].start()
+        mids.start()
+        ends[1].start()
+        laters = []
+        ends[0].wait()
+        laters.append(along(once(28), F.at[0, out, :], F.at[0, out_there, :], outer_row, x_pair[0]))
+        laters[-1].start()
+        for c in (1, 0):
+            firsts[c].wait()
+            laters.append(across(
+                once(30 + 2 * c), F.at[c, out_halo, one], F.at[c, out_halo, end_h],
+                F.at[c, out_halo, two], F.at[c, out_halo, top_h], z_first[c]))
+            laters[-1].start()
+        mids.wait()
+        laters.append(along(once(34), F.at[:, inn, :], F.at[:, inn_there, :], inner_row, inner_ok))
+        laters[-1].start()
+        ends[1].wait()
+        laters.append(along(once(29), F.at[1, out, :], F.at[1, out_there, :], outer_row, x_pair[1]))
+        laters[-1].start()
 
         def wait():
-            @pl.when(at > 0)
-            def _():
-                low.wait_send()
-                high.wait_recv()
-
-            @pl.when(at < count - 1)
-            def _():
-                high.wait_send()
-                low.wait_recv()
-
-        return start, wait
-
-    edges = (slice(0, h), slice(3 * h, 4 * h))
-    one, two, top_h, end_h = slice(h, 2 * h), slice(2 * h, 3 * h), slice(0, h), slice(3 * h, 4 * h)
-
-    def gather(F):
-        re_turn = both(8, F.at[0, own, one], F.at[0, own, end_h], F.at[0, own, two], F.at[0, own, top_h], 1)
-        im_turn = both(9, F.at[1, one, own], F.at[1, end_h, own], F.at[1, two, own], F.at[1, top_h, own], 0)
-        rest = [
-            both(10, F.at[0, one, own], F.at[0, end_h, own], F.at[0, two, own], F.at[0, top_h, own], 0),
-            both(11, F.at[1, own, one], F.at[1, own, end_h], F.at[1, own, two], F.at[1, own, top_h], 1),
-        ]
-        for start, _ in (re_turn, im_turn, *rest):
-            start()
-        re_turn[1]()
-        for q, e in enumerate(edges):
-            rest.append(both(12 + q, F.at[0, one, e], F.at[0, end_h, e], F.at[0, two, e], F.at[0, top_h, e], 0))
-            rest[-1][0]()
-        im_turn[1]()
-        for q, e in enumerate(edges):
-            rest.append(both(14 + q, F.at[1, e, one], F.at[1, e, end_h], F.at[1, e, two], F.at[1, e, top_h], 1))
-            rest[-1][0]()
-
-        def wait():
-            for _, done in rest:
-                done()
+            for swap in laters:
+                swap.wait()
 
         return wait
 
     load_r.wait()
-    gather_wait = gather(R)
+    spread_wait = spread(R)
 
     fill(G, every, every)
     fill(L, every, every)
@@ -169,7 +200,7 @@
         W[q] = sum(jnp.dot(part, pick, preferred_element_type=F32) for part in parts)
 
     load_m.wait()
-    gather_wait()
+    spread_wait()
 
     step = 32
 
@@ -187,7 +218,7 @@
         return "both"
 
     def patch(s, k, seen, acc):
-        X, Y = (XA, YA) if k == 0 else (XB, YB)
+        X, Y = XS[k], YS[k]
         a = off_ref[0, s] + h
         b = off_ref[1, s] + h
 
@@ -348,24 +379,13 @@
         acc = [jnp.zeros((8, side), F32)]
         timed = []
         for n, s in enumerate(order):
-            for q, stage in enumerate(patch(s, n % 2, seen, acc)):
+            for q, stage in enumerate(patch(s, n, seen, acc)):
                 timed.append((SKEW * n + q, n, stage))
         for _, _, stage in sorted(timed, key=lambda x: x[:2]):
             stage()
         acc = acc[0]
 
-        re_edge = [
-            both(q, S.at[0, top_h, e], RA.at[0, :, e], S.at[0, end_h, e], RA.at[1, :, e], 0)
-            for q, e in enumerate(edges)
-        ]
-        im_edge = [
-            both(2 + q, S.at[1, e, top_h], CC.at[0, e, :], S.at[1, e, end_h], CC.at[1, e, :], 1)
-            for q, e in enumerate(edges)
-        ]
-        re_mid = both(4, S.at[0, top_h, own], RA.at[0, :, own], S.at[0, end_h, own], RA.at[1, :, own], 0)
-        im_mid = both(5, S.at[1, own, top_h], CC.at[0, own, :], S.at[1, own, end_h], CC.at[1, own, :], 1)
-        for start, _ in (*re_edge, *im_edge, re_mid, im_mid):
-            start()
+        phase = lax.rem(it, 2)
         rr_l, pap_l = lanes(rr_acc), lanes(acc)
         T1[it, row] = jnp.where(ti == 0, rr_l, jnp.where(ti == 1, pap_l + RIDGE * rr_l, 0.0))
         ones = [
@@ -376,31 +396,81 @@
         ]
         for copy in ones:
             copy.start()
-        for _, done in re_edge:
-            done()
-
-        def add_rows(i, carry):
-            near = pl.ds(pl.multiple_of(i * 32, 32), 32)
-            for q in range(2):
-                rows = pl.ds(pl.multiple_of((1 + q) * h + i * 32, 32), 32)
-                for e in edges:
-                    S[0, rows, e] += RA[1 - q, near, e]
-            return carry
-        lax.fori_loop(0, h // 32, add_rows, 0)
-        re_turn = both(6, S.at[0, own, top_h], CA.at[0], S.at[0, own, end_h], CA.at[1], 1)
-        re_turn[0]()
-        for _, done in im_edge:
-            done()
-
-        def add_cols(i, carry):
-            for base in (0, 3 * h):
-                rows = pl.ds(pl.multiple_of(base + i * 32, 32), 32)
-                S[1, rows, one] += CC[1, rows, :]
-                S[1, rows, two] += CC[0, rows, :]
-            return carry
-        lax.fori_loop(0, h // 32, add_cols, 0)
-        im_turn = both(7, S.at[1, top_h, own], RC.at[0], S.at[1, end_h, own], RC.at[1], 0)
-        im_turn[0]()
+
+        fold_z = [
+            across(once(2 * c), S.at[c, outer, top_h], ZR.at[1, c], S.at[c, outer, end_h], ZR.at[0, c], z_first[c])
+            for c in range(2)
+        ]
+        fold_x = [along(once(4 + c), S.at[c, out_halo, :], RXO.at[c], outer_row, x_pair[c]) for c in range(2)]
+        fold_i = along(once(6), S.at[:, inn_halo, :], RXI, inner_row, inner_ok)
+        for swap in (fold_z[1], fold_z[0], fold_x[0], fold_i, fold_x[1]):
+            swap.start()
+
+        more = jnp.logical_not(last)
+
+        def meet(index, rows, buf, on):
+            def pick(c0, c1):
+                return S.at[:, rows, c0:c1] if buf is DXI else S.at[buf, rows, c0:c1]
+
+            def slot(from_side, c0, c1):
+                return DXI.at[phase, from_side, :, :, c0:c1] if buf is DXI else DXO.at[phase, from_side, buf, :, c0:c1]
+
+            full = across(turn(index, phase), pick(0, side), slot(1, 0, side), pick(side, 2 * side), slot(0, 0, side),
+                          jnp.logical_and(on, more))
+            part = across(turn(index, phase), pick(0, h), slot(1, 0, h), pick(3 * h, 4 * h), slot(0, h, side),
+                          jnp.logical_and(on, last))
+            return full, part
+
+        meet_i = meet(0, inn, DXI, yes)
+        meet_x = [meet(2 + 2 * c, out, c, x_first[c]) for c in range(2)]
+        meet_z = [
+            (
+                along(turn(6 + c, phase), S.at[c, outer, own], DZ.at[phase, c], outer_row,
+                      jnp.logical_and(z_first[c], more)),
+                along(turn(6 + c, phase), S.at[c, out_halo, own], DZ.at[phase, c, band(h * odd), :], outer_row,
+                      jnp.logical_and(z_first[c], last)),
+            )
+            for c in range(2)
+        ]
+
+        def begin(pair):
+            for swap in pair:
+                swap.start()
+
+        def end(pair):
+            for swap in pair:
+                swap.wait()
+
+        def rows_of(ref_rows, at):
+            return pl.ds(pl.multiple_of(ref_rows.start + at, 32), 32)
+
+        fold_i.wait()
+
+        @pl.when(inner_ok)
+        def _():
+            def add(at):
+                S[:, rows_of(inn, at), :] += RXI[:, pl.ds(at, 32), :]
+            chunks(h, 32, add)
+        begin(meet_i)
+        for c in (1, 0):
+            fold_z[c].wait()
+            for ok, cols, q in ((left_ok, one, 0), (right_ok, two, 1)):
+                @pl.when(jnp.logical_and(z_first[c], ok))
+                def _(c=c, cols=cols, q=q):
+                    def add(at):
+                        S[c, rows_of(outer, at), cols] += ZR[q, c, pl.ds(at, 32), :]
+                    chunks(side, 32, add)
+            begin(meet_z[c])
+        for c in range(2):
+            fold_x[c].wait()
+
+            @pl.when(x_pair[c])
+            def _(c=c):
+                def add(at):
+                    S[c, rows_of(out, at), :] += RXO[c, pl.ds(at, 32), :]
+                chunks(h, 32, add)
+            begin(meet_x[c])
+
         for copy in ones:
             copy.wait()
         total = T1[it, 0]
@@ -415,42 +485,69 @@
         ]
         for copy in twos:
             copy.start()
-        re_mid[1]()
-        im_mid[1]()
-        re_turn[1]()
-        im_turn[1]()
-
-        def make(i, carry):
-            near = pl.ds(pl.multiple_of(i * 32, 32), 32)
-            for q in range(2):
-                rows = pl.ds(pl.multiple_of((1 + q) * h + i * 32, 32), 32)
-                inner = pl.ds(pl.multiple_of(q * h + i * 32, 32), 32)
-                re = S[0, rows, own] + RA[1 - q, near, own]
-                im = S[1, rows, own] + RC[1 - q, near, :]
-                G[0, rows, one] = re[:, :h] + CA[1, inner, :]
-                G[0, rows, two] = re[:, h:] + CA[0, inner, :]
-                G[1, rows, one] = im[:, :h] + CC[1, rows, :]
-                G[1, rows, two] = im[:, h:] + CC[0, rows, :]
-            return carry
-        lax.fori_loop(0, h // 32, make, 0)
-
-        def scalars():
-            for copy in twos:
-                copy.wait()
-            total = T2[it, 0]
-            for q in range(1, n_col):
-                total = total + T2[it, q]
-            rr = jnp.sum(jnp.where(ti == 0, total, 0.0), keepdims=True)
-            pap = jnp.sum(jnp.where(ti == 1, total, 0.0), keepdims=True)
-            ratio = jnp.where(it == 0, 0.0, rr / rr_before)
-            return rr, ratio, rr / (pap - ratio * rr / alpha_before)
-
-        @pl.when(jnp.logical_not(last))
-        def _():
-            wait = gather(G)
-            wait()
-
-        rr, ratio, alpha = scalars()
+
+        def settle(c, rows, got):
+            def run(at):
+                here, there = rows_of(rows, at), pl.ds(at, 32)
+
+                @pl.when(left_ok)
+                def _():
+                    G[c, here, lefts] = S[c, here, lefts] + got(0, there)
+
+                @pl.when(right_ok)
+                def _():
+                    G[c, here, rights] = S[c, here, rights] + got(1, there)
+
+                @pl.when(jnp.logical_not(left_ok))
+                def _():
+                    G[c, here, one] = S[c, here, one]
+
+                @pl.when(jnp.logical_not(right_ok))
+                def _():
+                    G[c, here, two] = S[c, here, two]
+            chunks(h, 32, run)
+
+        share_i = along(once(8), G.at[:, inn, :], G.at[:, inn_there, :], inner_row, jnp.logical_and(inner_ok, more))
+        share_x = [
+            along(once(10 + c), G.at[c, out, :], G.at[c, out_there, :], outer_row, jnp.logical_and(x_pair[c], more))
+            for c in range(2)
+        ]
+        share_z = [
+            across(once(12 + 2 * c), G.at[c, outer, one], G.at[c, outer, end_h], G.at[c, outer, two],
+                   G.at[c, outer, top_h], jnp.logical_and(z_first[c], more))
+            for c in range(2)
+        ]
+        end(meet_i)
+        for c in range(2):
+            settle(c, inn, lambda q, there, c=c: DXI[phase, q, c, there, :])
+        share_i.start()
+        for c in range(2):
+            end(meet_x[c])
+
+            @pl.when(x_first[c])
+            def _(c=c):
+                settle(c, out, lambda q, there: DXO[phase, q, c, there, :])
+            share_x[c].start()
+        for c in (1, 0):
+            end(meet_z[c])
+
+            @pl.when(z_first[c])
+            def _(c=c):
+                def run(at):
+                    here = rows_of(outer, at)
+                    G[c, here, own] = S[c, here, own] + DZ[phase, c, pl.ds(at, 32), :]
+                chunks(side, 32, run)
+            share_z[c].start()
+
+        for copy in twos:
+            copy.wait()
+        total = T2[it, 0]
+        for q in range(1, n_col):
+            total = total + T2[it, q]
+        rr = jnp.sum(jnp.where(ti == 0, total, 0.0), keepdims=True)
+        pap = jnp.sum(jnp.where(ti == 1, total, 0.0), keepdims=True)
+        ratio = jnp.where(it == 0, 0.0, rr / rr_before)
+        alpha = rr / (pap - ratio * rr / alpha_before)
 
         def advance(i, carry):
             near = pl.ds(pl.multiple_of(i * 32, 32), 32)
@@ -462,25 +559,38 @@
             return carry
         lax.fori_loop(0, side // 32, advance, 0)
 
-        def advance_r(rows):
-            for c in range(2):
-                r = R[c, rows, :]
-                along = G[c, rows, :] + RIDGE * r + ratio * L[c, rows, :]
-                L[c, rows, :] = along
-                R[c, rows, :] = r - alpha * along
-        chunks(2 * side, 32, advance_r)
+        for swap in (share_i, *share_x, *share_z):
+            swap.wait()
+
+        @pl.when(more)
+        def _():
+            def advance_r(at):
+                rows = pl.ds(at, 32)
+                for c in range(2):
+                    r = R[c, rows, :]
+                    image = G[c, rows, :] + RIDGE * r + ratio * L[c, rows, :]
+                    L[c, rows, :] = image
+                    R[c, rows, :] = r - alpha * image
+            chunks(2 * side, 32, advance_r)
+
+        @pl.when(last)
+        def _():
+            def emit(at):
+                rows = pl.ds(pl.multiple_of(h + at, 32), 32)
+                for c in range(2):
+                    r = R[c, rows, own]
+                    image = G[c, rows, own] + RIDGE * r + ratio * L[c, rows, own]
+                    res_ref[c, pl.ds(at, 32), :] = r - alpha * image
+            chunks(side, 32, emit)
         return alpha, rr
 
     one11 = jnp.ones((1, 1), F32)
     lax.fori_loop(0, ITERS, iteration, (one11, one11))
 
-    def emit(rows):
-        res_ref[:, rows, :] = R[:, pl.ds(pl.multiple_of(rows.start + h, 32), 32), own]
-    chunks(side, 32, emit)
-
 
 def solution(mesh):
     n_row, n_col = mesh.shape["row"], mesh.shape["col"]
+    n_x = len({tuple(getattr(d, "coords", (d.id,)))[0] for d in mesh.devices.flat})
 
     def local(right_side, probe, weights, offsets, counts):
         side = probe.shape[1]
@@ -495,7 +605,7 @@
         dma = pltpu.SemaphoreType.DMA
         vmem = pl.BlockSpec(memory_space=pltpu.VMEM)
         return pl.pallas_call(
-            functools.partial(kernel, n_row, n_col, cap, side),
+            functools.partial(kernel, n_row, n_col, n_x, cap, side),
             out_shape=(block, block),
             in_specs=[smem, smem, hbm, hbm, hbm, hbm],
             out_specs=(vmem, vmem),
@@ -506,18 +616,18 @@
                 tile,
                 pltpu.VMEM((side, side), F32),
                 pltpu.VMEM((8, side, side), BF16),
-                pltpu.VMEM((4, 2, side, side), BF16),
-                pltpu.VMEM((4, 2, side, side), BF16),
-                pltpu.VMEM((4, side, side), F32),
-                pltpu.VMEM((4, side, side), F32),
+                [pltpu.VMEM((4, 2, side, side), BF16) for _ in range(cap)],
+                [pltpu.VMEM((4, side, side), F32) for _ in range(cap)],
                 tile,
                 pltpu.VMEM((2, h, 2 * side), F32),
-                pltpu.VMEM((2, side, h), F32),
-                pltpu.VMEM((2, 2 * side, h), F32),
-                pltpu.VMEM((2, h, side), F32),
+                pltpu.VMEM((2, h, 2 * side), F32),
+                pltpu.VMEM((2, 2, 2, h, side), F32),
+                pltpu.VMEM((2, 2, 2, h, side), F32),
+                pltpu.VMEM((2, 2, side, h), F32),
+                pltpu.VMEM((2, 2, side, side), F32),
                 pltpu.VMEM((ITERS, n_row, 8, 128), F32),
                 pltpu.VMEM((ITERS, n_col, 8, 128), F32),
-                dma((32,)), dma((32,)),
+                dma((36,)), dma((36,)), dma((2, 8)), dma((2, 8)),
                 dma((ITERS, n_row)), dma((ITERS, n_row)),
                 dma((ITERS, n_col)), dma((ITERS, n_col)),
                 dma((4,)),

time: 93.9 us -> 86.4 us (0.920); the launches traced: 92 us -> 86.3 us
  Pallas kernels: 87.5 us -> 81.8 us
    pallas_call x1, Pallas kernels: 87.5 us -> 81.8 us  [local(): pl.pallas_call(functools.partial(kernel, n_row, n_col, n_x, cap, side), o...]
where the time goes in v2:
time: 86.4 us; the launch traced here: 86.3 us
  Pallas kernels  81.8 us (95%)
  local copies, waits for them, and re-layouts  3.21 us (4%)
  between operations  1.3 us (2%)
    pallas_call x1, Pallas kernels, local(): pl.pallas_call(functools.partial(kernel, n_row, n_col, n_x, cap, side), o...  81.8 us
    unnamed x6, local copies, waits for them, and re-layouts  3.21 us

profile of v2, /device:TPU:4, one launch (start us, length us, event | category | flops | bytes accessed | tf_op | source)
XLA Modules:
  0.0 86.3 jit_solution(9246083313549128770)
XLA Ops:
  1.3 0.0 copy-start.1
  1.3 0.7 copy-done.1
  2.0 0.0 copy-start
  2.0 0.9 %copy-done = f32[256,256]{1,0:T(8,128)S(1)} copy-done((f32[256,256]{1,0:T(8,128)S(1)}, f32[256,256]{1,0:T(8,128)}, u32[]{:S(2)}) %copy-start) | copy-done | bytes 262168
  2.9 81.8 %shard_map.77 = (f32[2,256,256]{2,1,0:T(8,128)S(1)}, f32[2,256,256]{2,1,0:T(8,128)S(1)}) custom-call(s32[2,4]{1,0:T(2,128)S(1)} %bitcast.3, s32[1,1]{1,0:T(1,128)S(6)} %copy.10.cnt_ref, f32[2,256,256]{2,1,0:T(8,128)} %rhs_hbm.1, f32[2,256,256]{2,1,0:T(8,128)} %probe_hbm.1, f32[256,256]{1,0:T(8,128)S(1)} %copy-done, bf16[8,256,256]{2,1,0:T(8,128)(2,1)} %constant.2.clone.mat_hbm), custom_call_target="tpu_custom_call" | custom-call | tf_op jit(solution)/shard_map/pallas_call | solution.py:607
  84.7 0.8 copy.11
  85.5 0.8 copy.12
Async XLA Ops:
  1.3 0.7 copy-start.1
  2.0 0.9 %copy-start = (f32[256,256]{1,0:T(8,128)S(1)}, f32[256,256]{1,0:T(8,128)}, u32[]{:S(2)}) copy-start(f32[256,256]{1,0:T(8,128)} %w_hbm.1) | copy-start | bytes 786436

commit v3 on v2

--- a/solution.py
+++ b/solution.py
@@ -126,18 +126,24 @@
             (left_src, left_dst, (row, col - 1), go_left, go_right),
             (right_src, right_dst, (row, col + 1), go_right, go_left)])
 
-    def along(sems, src, dst, there, on):
-        return Swap(sems, [(src, dst, (there, col), on, on)])
+    def leftward(sems, src, dst, on):
+        return Swap(sems, [(src, dst, (row, col - 1), jnp.logical_and(on, left_ok), jnp.logical_and(on, right_ok))])
+
+    def rightward(sems, src, dst, on):
+        return Swap(sems, [(src, dst, (row, col + 1), jnp.logical_and(on, right_ok), jnp.logical_and(on, left_ok))])
+
+    def along(sems, src, dst, there, on, gets=None):
+        return Swap(sems, [(src, dst, (there, col), on, on if gets is None else gets)])
 
     yes = col >= 0
 
     def spread(F):
         ends = [
-            across(once(20 + 2 * c), F.at[c, out, one], F.at[c, out, end_h], F.at[c, out, two], F.at[c, out, top_h], yes)
+            across(once(30 + 2 * c), F.at[c, out, one], F.at[c, out, end_h], F.at[c, out, two], F.at[c, out, top_h], yes)
             for c in range(2)
         ]
-        mids = across(once(24), F.at[:, inn, one], F.at[:, inn, end_h], F.at[:, inn, two], F.at[:, inn, top_h], yes)
-        firsts = [along(once(26 + c), F.at[c, out, own], F.at[c, out_there, own], outer_row, z_first[c]) for c in range(2)]
+        mids = across(once(34), F.at[:, inn, one], F.at[:, inn, end_h], F.at[:, inn, two], F.at[:, inn, top_h], yes)
+        firsts = [along(once(36 + c), F.at[c, out, own], F.at[c, out_there, own], outer_row, z_first[c]) for c in range(2)]
         ends[0].start()
         firsts[1].start()
         firsts[0].start()
@@ -145,19 +151,19 @@
         ends[1].start()
         laters = []
         ends[0].wait()
-        laters.append(along(once(28), F.at[0, out, :], F.at[0, out_there, :], outer_row, x_pair[0]))
+        laters.append(along(once(38), F.at[0, out, :], F.at[0, out_there, :], outer_row, x_pair[0]))
         laters[-1].start()
         for c in (1, 0):
             firsts[c].wait()
             laters.append(across(
-                once(30 + 2 * c), F.at[c, out_halo, one], F.at[c, out_halo, end_h],
+                once(40 + 2 * c), F.at[c, out_halo, one], F.at[c, out_halo, end_h],
                 F.at[c, out_halo, two], F.at[c, out_halo, top_h], z_first[c]))
             laters[-1].start()
         mids.wait()
-        laters.append(along(once(34), F.at[:, inn, :], F.at[:, inn_there, :], inner_row, inner_ok))
+        laters.append(along(once(44), F.at[:, inn, :], F.at[:, inn_there, :], inner_row, inner_ok))
         laters[-1].start()
         ends[1].wait()
-        laters.append(along(once(29), F.at[1, out, :], F.at[1, out_there, :], outer_row, x_pair[1]))
+        laters.append(along(once(39), F.at[1, out, :], F.at[1, out_there, :], outer_row, x_pair[1]))
         laters[-1].start()
 
         def wait():
@@ -357,8 +363,6 @@
 
         return [load, mul_a, mix_b, mul_b, mix_c, mul_c, mix_d, mul_d, store]
 
-    ti = lax.broadcasted_iota(jnp.int32, (8, 128), 0)
-
     def lanes(acc):
         total = acc[:, 0:128]
         for q in range(128, acc.shape[1], 128):
@@ -387,7 +391,7 @@
 
         phase = lax.rem(it, 2)
         rr_l, pap_l = lanes(rr_acc), lanes(acc)
-        T1[it, row] = jnp.where(ti == 0, rr_l, jnp.where(ti == 1, pap_l + RIDGE * rr_l, 0.0))
+        T1[it, row] = jnp.concatenate([rr_l, pap_l + RIDGE * rr_l], 0)
         ones = [
             pltpu.make_async_remote_copy(
                 src_ref=T1.at[it, row], dst_ref=T1.at[it, row], send_sem=s1_send.at[it, d],
@@ -397,41 +401,60 @@
         for copy in ones:
             copy.start()
 
-        fold_z = [
-            across(once(2 * c), S.at[c, outer, top_h], ZR.at[1, c], S.at[c, outer, end_h], ZR.at[0, c], z_first[c])
-            for c in range(2)
+        more = jnp.logical_not(last)
+
+        def rows_of(ref_rows, at):
+            return pl.ds(pl.multiple_of(ref_rows.start + at, 32), 32)
+
+        def strip(q):
+            return band((2 * odd + q) * h)
+
+        halves = (lefts, rights)
+        pieces = [(c, q) for c in (1, 0) for q in range(2)]
+        fold_z = {
+            (c, q): across(
+                once(4 * c + 2 * q), S.at[c, strip(q), top_h], ZR.at[1, c, q], S.at[c, strip(q), end_h],
+                ZR.at[0, c, q], z_first[c])
+            for c, q in pieces
+        }
+        fold_x = {
+            (c, p): along(once(8 + 2 * c + p), S.at[c, out_halo, halves[p]], RXO.at[c, p], outer_row, x_pair[c])
+            for c in range(2) for p in range(2)
+        }
+        fold_i = along(once(12), S.at[:, inn_halo, :], RXI, inner_row, inner_ok)
+        fold_z[1, 0].start()
+        fold_x[0, 0].start()
+        fold_x[0, 1].start()
+        fold_i.start()
+        for key in pieces[1:]:
+            fold_z[key].start()
+        fold_x[1, 0].start()
+        fold_x[1, 1].start()
+
+        def meet(index, src, buf, on):
+            def slot(p, c0, c1):
+                return buf.at[(phase, p) + (slice(None),) * (len(buf.shape) - 3) + (slice(c0, c1),)]
+
+            full, part = jnp.logical_and(on, more), jnp.logical_and(on, last)
+            to_left = (
+                leftward(turn(index, phase), src(0, side), slot(1, 0, side), full),
+                leftward(turn(index, phase), src(0, h), slot(1, 0, h), part))
+            to_right = (
+                rightward(turn(index + 1, phase), src(side, 2 * side), slot(0, 0, side), full),
+                rightward(turn(index + 1, phase), src(3 * h, 4 * h), slot(0, h, side), part))
+            return to_left, to_right
+
+        meet_i = meet(0, lambda c0, c1: S.at[:, inn, c0:c1], DXI, yes)
+        meet_x = [
+            meet(2 + 2 * c, lambda c0, c1, c=c: S.at[c, out, c0:c1], DXO[c], x_first[c]) for c in range(2)
         ]
-        fold_x = [along(once(4 + c), S.at[c, out_halo, :], RXO.at[c], outer_row, x_pair[c]) for c in range(2)]
-        fold_i = along(once(6), S.at[:, inn_halo, :], RXI, inner_row, inner_ok)
-        for swap in (fold_z[1], fold_z[0], fold_x[0], fold_i, fold_x[1]):
-            swap.start()
-
-        more = jnp.logical_not(last)
-
-        def meet(index, rows, buf, on):
-            def pick(c0, c1):
-                return S.at[:, rows, c0:c1] if buf is DXI else S.at[buf, rows, c0:c1]
-
-            def slot(from_side, c0, c1):
-                return DXI.at[phase, from_side, :, :, c0:c1] if buf is DXI else DXO.at[phase, from_side, buf, :, c0:c1]
-
-            full = across(turn(index, phase), pick(0, side), slot(1, 0, side), pick(side, 2 * side), slot(0, 0, side),
-                          jnp.logical_and(on, more))
-            part = across(turn(index, phase), pick(0, h), slot(1, 0, h), pick(3 * h, 4 * h), slot(0, h, side),
-                          jnp.logical_and(on, last))
-            return full, part
-
-        meet_i = meet(0, inn, DXI, yes)
-        meet_x = [meet(2 + 2 * c, out, c, x_first[c]) for c in range(2)]
-        meet_z = [
-            (
-                along(turn(6 + c, phase), S.at[c, outer, own], DZ.at[phase, c], outer_row,
-                      jnp.logical_and(z_first[c], more)),
-                along(turn(6 + c, phase), S.at[c, out_halo, own], DZ.at[phase, c, band(h * odd), :], outer_row,
-                      jnp.logical_and(z_first[c], last)),
-            )
-            for c in range(2)
-        ]
+        meet_z = {
+            (c, q): along(
+                turn(6 + 2 * c + q, phase), S.at[c, strip(q), own], DZ.at[phase, c, q], outer_row,
+                jnp.logical_and(z_first[c], jnp.logical_or(more, odd == q)),
+                jnp.logical_and(z_first[c], jnp.logical_or(more, odd != q)))
+            for c, q in pieces
+        }
 
         def begin(pair):
             for swap in pair:
@@ -440,9 +463,6 @@
         def end(pair):
             for swap in pair:
                 swap.wait()
-
-        def rows_of(ref_rows, at):
-            return pl.ds(pl.multiple_of(ref_rows.start + at, 32), 32)
 
         fold_i.wait()
 
@@ -451,26 +471,33 @@
             def add(at):
                 S[:, rows_of(inn, at), :] += RXI[:, pl.ds(at, 32), :]
             chunks(h, 32, add)
-        begin(meet_i)
-        for c in (1, 0):
-            fold_z[c].wait()
-            for ok, cols, q in ((left_ok, one, 0), (right_ok, two, 1)):
+        begin(meet_i[0])
+        begin(meet_i[1])
+
+        def turn_z(c, q):
+            fold_z[c, q].wait()
+            for ok, cols, side_q in ((left_ok, one, 0), (right_ok, two, 1)):
                 @pl.when(jnp.logical_and(z_first[c], ok))
-                def _(c=c, cols=cols, q=q):
+                def _():
                     def add(at):
-                        S[c, rows_of(outer, at), cols] += ZR[q, c, pl.ds(at, 32), :]
-                    chunks(side, 32, add)
-            begin(meet_z[c])
-        for c in range(2):
-            fold_x[c].wait()
-
-            @pl.when(x_pair[c])
-            def _(c=c):
-                def add(at):
-                    S[c, rows_of(out, at), :] += RXO[c, pl.ds(at, 32), :]
-                chunks(h, 32, add)
-            begin(meet_x[c])
-
+                        S[c, rows_of(strip(q), at), cols] += ZR[side_q, c, q, pl.ds(at, 32), :]
+                    chunks(h, 32, add)
+            meet_z[c, q].start()
+
+        def turn_x(c):
+            for p in range(2):
+                fold_x[c, p].wait()
+
+                @pl.when(x_pair[c])
+                def _():
+                    def add(at):
+                        S[c, rows_of(out, at), halves[p]] += RXO[c, p, pl.ds(at, 32), :]
+                    chunks(h, 32, add)
+                begin(meet_x[c][p])
+
+        turn_z(*pieces[0])
+        turn_z(*pieces[1])
+        turn_x(0)
         for copy in ones:
             copy.wait()
         total = T1[it, 0]
@@ -485,67 +512,79 @@
         ]
         for copy in twos:
             copy.start()
-
-        def settle(c, rows, got):
-            def run(at):
-                here, there = rows_of(rows, at), pl.ds(at, 32)
-
-                @pl.when(left_ok)
-                def _():
-                    G[c, here, lefts] = S[c, here, lefts] + got(0, there)
-
-                @pl.when(right_ok)
-                def _():
-                    G[c, here, rights] = S[c, here, rights] + got(1, there)
-
-                @pl.when(jnp.logical_not(left_ok))
-                def _():
-                    G[c, here, one] = S[c, here, one]
-
-                @pl.when(jnp.logical_not(right_ok))
-                def _():
-                    G[c, here, two] = S[c, here, two]
-            chunks(h, 32, run)
-
-        share_i = along(once(8), G.at[:, inn, :], G.at[:, inn_there, :], inner_row, jnp.logical_and(inner_ok, more))
-        share_x = [
-            along(once(10 + c), G.at[c, out, :], G.at[c, out_there, :], outer_row, jnp.logical_and(x_pair[c], more))
-            for c in range(2)
-        ]
-        share_z = [
-            across(once(12 + 2 * c), G.at[c, outer, one], G.at[c, outer, end_h], G.at[c, outer, two],
-                   G.at[c, outer, top_h], jnp.logical_and(z_first[c], more))
-            for c in range(2)
-        ]
-        end(meet_i)
-        for c in range(2):
-            settle(c, inn, lambda q, there, c=c: DXI[phase, q, c, there, :])
-        share_i.start()
-        for c in range(2):
-            end(meet_x[c])
+        turn_z(*pieces[2])
+        turn_z(*pieces[3])
+        turn_x(1)
+
+        def settle(c, rows, p, got):
+            ok, cols, mine = ((left_ok, lefts, one), (right_ok, rights, two))[p]
+
+            @pl.when(ok)
+            def _():
+                def run(at):
+                    here = rows_of(rows, at)
+                    G[c, here, cols] = S[c, here, cols] + got(pl.ds(at, 32))
+                chunks(h, 32, run)
+
+            @pl.when(jnp.logical_not(ok))
+            def _():
+                def run(at):
+                    here = rows_of(rows, at)
+                    G[c, here, mine] = S[c, here, mine]
+                chunks(h, 32, run)
+
+        shares = []
+
+        def share(swap):
+            swap.start()
+            shares.append(swap)
+
+        def done_i(p):
+            end(meet_i[1 - p])
+            for c in range(2):
+                settle(c, inn, p, lambda there, c=c: DXI[phase, p, c, there, :])
+            share(along(once(16 + p), G.at[:, inn, halves[p]], G.at[:, inn_there, halves[p]], inner_row,
+                        jnp.logical_and(inner_ok, more)))
+
+        def done_x(c, p):
+            end(meet_x[c][1 - p])
 
             @pl.when(x_first[c])
-            def _(c=c):
-                settle(c, out, lambda q, there: DXO[phase, q, c, there, :])
-            share_x[c].start()
-        for c in (1, 0):
-            end(meet_z[c])
+            def _():
+                settle(c, out, p, lambda there: DXO[c][phase, p, there, :])
+            share(along(once(18 + 2 * c + p), G.at[c, out, halves[p]], G.at[c, out_there, halves[p]], outer_row,
+                        jnp.logical_and(x_pair[c], more)))
+
+        def done_z(c, q):
+            meet_z[c, q].wait()
 
             @pl.when(z_first[c])
-            def _(c=c):
+            def _():
                 def run(at):
-                    here = rows_of(outer, at)
-                    G[c, here, own] = S[c, here, own] + DZ[phase, c, pl.ds(at, 32), :]
-                chunks(side, 32, run)
-            share_z[c].start()
+                    here = rows_of(strip(q), at)
+                    G[c, here, own] = S[c, here, own] + DZ[phase, c, q, pl.ds(at, 32), :]
+                chunks(h, 32, run)
+            share(across(
+                once(22 + 4 * c + 2 * q), G.at[c, strip(q), one], G.at[c, strip(q), end_h],
+                G.at[c, strip(q), two], G.at[c, strip(q), top_h], jnp.logical_and(z_first[c], more)))
+
+        done_z(*pieces[0])
+        done_i(0)
+        done_i(1)
+        done_x(0, 0)
+        done_x(0, 1)
+        for key in pieces[1:]:
+            done_z(*key)
+        done_x(1, 0)
+        done_x(1, 1)
 
         for copy in twos:
             copy.wait()
         total = T2[it, 0]
         for q in range(1, n_col):
             total = total + T2[it, q]
-        rr = jnp.sum(jnp.where(ti == 0, total, 0.0), keepdims=True)
-        pap = jnp.sum(jnp.where(ti == 1, total, 0.0), keepdims=True)
+        rr = jnp.sum(total[0:1], keepdims=True)
+        pap = jnp.sum(total[1:2], keepdims=True)
         ratio = jnp.where(it == 0, 0.0, rr / rr_before)
         alpha = rr / (pap - ratio * rr / alpha_before)
 
@@ -559,7 +598,7 @@
             return carry
         lax.fori_loop(0, side // 32, advance, 0)
 
-        for swap in (share_i, *share_x, *share_z):
+        for swap in shares:
             swap.wait()
 
         @pl.when(more)
@@ -620,14 +659,14 @@
                 [pltpu.VMEM((4, side, side), F32) for _ in range(cap)],
                 tile,
                 pltpu.VMEM((2, h, 2 * side), F32),
-                pltpu.VMEM((2, h, 2 * side), F32),
+                pltpu.VMEM((2, 2, h, side), F32),
                 pltpu.VMEM((2, 2, 2, h, side), F32),
+                [pltpu.VMEM((2, 2, h, side), F32) for _ in range(2)],
+                pltpu.VMEM((2, 2, 2, h, h), F32),
                 pltpu.VMEM((2, 2, 2, h, side), F32),
-                pltpu.VMEM((2, 2, side, h), F32),
-                pltpu.VMEM((2, 2, side, side), F32),
-                pltpu.VMEM((ITERS, n_row, 8, 128), F32),
-                pltpu.VMEM((ITERS, n_col, 8, 128), F32),
-                dma((36,)), dma((36,)), dma((2, 8)), dma((2, 8)),
+                pltpu.VMEM((ITERS, n_row, 2, 128), F32),
+                pltpu.VMEM((ITERS, n_col, 2, 128), F32),
+                dma((48,)), dma((48,)), dma((2, 10)), dma((2, 10)),
                 dma((ITERS, n_row)), dma((ITERS, n_row)),
                 dma((ITERS, n_col)), dma((ITERS, n_col)),
                 dma((4,)),

time: 86.4 us -> 83.6 us (0.968); the launches traced: 86.3 us -> 82.4 us
  Pallas kernels: 81.8 us -> 77.9 us
    pallas_call x1, Pallas kernels: 81.8 us -> 77.9 us  [local(): pl.pallas_call(functools.partial(kernel, n_row, n_col, n_x, cap, side), o...]
where the time goes in v3:
time: 83.6 us; the launch traced here: 82.4 us
  Pallas kernels  77.9 us (93%)
  local copies, waits for them, and re-layouts  3.21 us (4%)
  between operations  1.3 us (2%)
    pallas_call x1, Pallas kernels, local(): pl.pallas_call(functools.partial(kernel, n_row, n_col, n_x, cap, side), o...  77.9 us
    unnamed x6, local copies, waits for them, and re-layouts  3.21 us

profile of v3, /device:TPU:4, one launch (start us, length us, event | category | flops | bytes accessed | tf_op | source)
XLA Modules:
  0.0 82.4 jit_solution(3603136160193805970)
XLA Ops:
  1.3 0.0 copy-start.1
  1.3 0.7 copy-done.1
  2.0 0.0 copy-start
  2.0 0.9 %copy-done = f32[256,256]{1,0:T(8,128)S(1)} copy-done((f32[256,256]{1,0:T(8,128)S(1)}, f32[256,256]{1,0:T(8,128)}, u32[]{:S(2)}) %copy-start) | copy-done | bytes 262168
  2.9 77.9 %shard_map.77 = (f32[2,256,256]{2,1,0:T(8,128)S(1)}, f32[2,256,256]{2,1,0:T(8,128)S(1)}) custom-call(s32[2,4]{1,0:T(2,128)S(1)} %bitcast.3, s32[1,1]{1,0:T(1,128)S(6)} %copy.10.cnt_ref, f32[2,256,256]{2,1,0:T(8,128)} %rhs_hbm.1, f32[2,256,256]{2,1,0:T(8,128)} %probe_hbm.1, f32[256,256]{1,0:T(8,128)S(1)} %copy-done, bf16[8,256,256]{2,1,0:T(8,128)(2,1)} %constant.2.clone.mat_hbm), custom_call_target="tpu_custom_call" | custom-call | tf_op jit(solution)/shard_map/pallas_call | solution.py:646
  80.9 0.8 copy.11
  81.7 0.8 copy.12
Async XLA Ops:
  1.3 0.7 copy-start.1
  2.0 0.9 %copy-start = (f32[256,256]{1,0:T(8,128)S(1)}, f32[256,256]{1,0:T(8,128)}, u32[]{:S(2)}) copy-start(f32[256,256]{1,0:T(8,128)} %w_hbm.1) | copy-start | bytes 786436

commit v4 on v3

--- a/solution.py
+++ b/solution.py
@@ -11,7 +11,8 @@
 
 ITERS = 3
 RIDGE = 0.5
-SKEW = 1.0
+SKEW = 0.1
+STRIPS = 2
 MESH = pl.DeviceIdType.MESH
 F32 = jnp.float32
 BF16 = jnp.bfloat16
@@ -163,8 +164,6 @@
         laters.append(along(once(44), F.at[:, inn, :], F.at[:, inn_there, :], inner_row, inner_ok))
         laters[-1].start()
         ends[1].wait()
-        laters.append(along(once(39), F.at[1, out, :], F.at[1, out_there, :], outer_row, x_pair[1]))
-        laters[-1].start()
 
         def wait():
             for swap in laters:
@@ -406,20 +405,22 @@
         def rows_of(ref_rows, at):
             return pl.ds(pl.multiple_of(ref_rows.start + at, 32), 32)
 
+        tall = side // STRIPS
+
         def strip(q):
-            return band((2 * odd + q) * h)
+            return pl.ds(pl.multiple_of(2 * h * odd + q * tall, tall), tall)
 
         halves = (lefts, rights)
-        pieces = [(c, q) for c in (1, 0) for q in range(2)]
+        pieces = [(c, q) for c in (1, 0) for q in range(STRIPS)]
         fold_z = {
             (c, q): across(
-                once(4 * c + 2 * q), S.at[c, strip(q), top_h], ZR.at[1, c, q], S.at[c, strip(q), end_h],
+                once(48 + 2 * (c * STRIPS + q)), S.at[c, strip(q), top_h], ZR.at[1, c, q], S.at[c, strip(q), end_h],
                 ZR.at[0, c, q], z_first[c])
             for c, q in pieces
         }
         fold_x = {
             (c, p): along(once(8 + 2 * c + p), S.at[c, out_halo, halves[p]], RXO.at[c, p], outer_row, x_pair[c])
-            for c in range(2) for p in range(2)
+            for c in range(1) for p in range(2)
         }
         fold_i = along(once(12), S.at[:, inn_halo, :], RXI, inner_row, inner_ok)
         fold_z[1, 0].start()
@@ -428,8 +429,6 @@
         fold_i.start()
         for key in pieces[1:]:
             fold_z[key].start()
-        fold_x[1, 0].start()
-        fold_x[1, 1].start()
 
         def meet(index, src, buf, on):
             def slot(p, c0, c1):
@@ -450,9 +449,9 @@
         ]
         meet_z = {
             (c, q): along(
-                turn(6 + 2 * c + q, phase), S.at[c, strip(q), own], DZ.at[phase, c, q], outer_row,
-                jnp.logical_and(z_first[c], jnp.logical_or(more, odd == q)),
-                jnp.logical_and(z_first[c], jnp.logical_or(more, odd != q)))
+                turn(6 + c * STRIPS + q, phase), S.at[c, strip(q), own], DZ.at[phase, c, q], outer_row,
+                jnp.logical_and(z_first[c], jnp.logical_or(more, odd == 2 * q // STRIPS)),
+                jnp.logical_and(z_first[c], jnp.logical_or(more, odd != 2 * q // STRIPS)))
             for c, q in pieces
         }
 
@@ -481,22 +480,23 @@
                 def _():
                     def add(at):
                         S[c, rows_of(strip(q), at), cols] += ZR[side_q, c, q, pl.ds(at, 32), :]
-                    chunks(h, 32, add)
+                    chunks(tall, 32, add)
             meet_z[c, q].start()
 
         def turn_x(c):
             for p in range(2):
-                fold_x[c, p].wait()
-
-                @pl.when(x_pair[c])
-                def _():
-                    def add(at):
-                        S[c, rows_of(out, at), halves[p]] += RXO[c, p, pl.ds(at, 32), :]
-                    chunks(h, 32, add)
+                if c == 0:
+                    fold_x[c, p].wait()
+
+                    @pl.when(x_pair[c])
+                    def _():
+                        def add(at):
+                            S[c, rows_of(out, at), halves[p]] += RXO[c, p, pl.ds(at, 32), :]
+                        chunks(h, 32, add)
                 begin(meet_x[c][p])
 
-        turn_z(*pieces[0])
-        turn_z(*pieces[1])
+        for key in pieces[:STRIPS]:
+            turn_z(*key)
         turn_x(0)
         for copy in ones:
             copy.wait()
@@ -512,8 +512,8 @@
         ]
         for copy in twos:
             copy.start()
-        turn_z(*pieces[2])
-        turn_z(*pieces[3])
+        for key in pieces[STRIPS:]:
+            turn_z(*key)
         turn_x(1)
 
         def settle(c, rows, p, got):
@@ -552,8 +552,9 @@
             @pl.when(x_first[c])
             def _():
                 settle(c, out, p, lambda there: DXO[c][phase, p, there, :])
-            share(along(once(18 + 2 * c + p), G.at[c, out, halves[p]], G.at[c, out_there, halves[p]], outer_row,
-                        jnp.logical_and(x_pair[c], more)))
+            if c == 0:
+                share(along(once(18 + 2 * c + p), G.at[c, out, halves[p]], G.at[c, out_there, halves[p]], outer_row,
+                            jnp.logical_and(x_pair[c], more)))
 
         def done_z(c, q):
             meet_z[c, q].wait()
@@ -563,17 +564,18 @@
                 def run(at):
                     here = rows_of(strip(q), at)
                     G[c, here, own] = S[c, here, own] + DZ[phase, c, q, pl.ds(at, 32), :]
-                chunks(h, 32, run)
+                chunks(tall, 32, run)
             share(across(
-                once(22 + 4 * c + 2 * q), G.at[c, strip(q), one], G.at[c, strip(q), end_h],
+                once(48 + 4 * STRIPS + 2 * (c * STRIPS + q)), G.at[c, strip(q), one], G.at[c, strip(q), end_h],
                 G.at[c, strip(q), two], G.at[c, strip(q), top_h], jnp.logical_and(z_first[c], more)))
 
-        done_z(*pieces[0])
+        for key in pieces[:STRIPS]:
+            done_z(*key)
         done_i(0)
         done_i(1)
         done_x(0, 0)
         done_x(0, 1)
-        for key in pieces[1:]:
+        for key in pieces[STRIPS:]:
             done_z(*key)
         done_x(1, 0)
         done_x(1, 1)
@@ -588,6 +590,13 @@
         ratio = jnp.where(it == 0, 0.0, rr / rr_before)
         alpha = rr / (pap - ratio * rr / alpha_before)
 
+        def update(rows, cols):
+            for c in range(2):
+                r = R[c, rows, cols]
+                image = G[c, rows, cols] + RIDGE * r + ratio * L[c, rows, cols]
+                L[c, rows, cols] = image
+                R[c, rows, cols] = r - alpha * image
+
         def advance(i, carry):
             near = pl.ds(pl.multiple_of(i * 32, 32), 32)
             rows = pl.ds(pl.multiple_of(h + i * 32, 32), 32)
@@ -598,19 +607,24 @@
             return carry
         lax.fori_loop(0, side // 32, advance, 0)
 
+        @pl.when(more)
+        def _():
+            def advance_own(at):
+                rows = pl.ds(pl.multiple_of(h + at, 32), 32)
+                update(rows, own)
+            chunks(side, 32, advance_own)
         for swap in shares:
             swap.wait()
 
         @pl.when(more)
         def _():
             def advance_r(at):
-                rows = pl.ds(at, 32)
-                for c in range(2):
-                    r = R[c, rows, :]
-                    image = G[c, rows, :] + RIDGE * r + ratio * L[c, rows, :]
-                    L[c, rows, :] = image
-                    R[c, rows, :] = r - alpha * image
-            chunks(2 * side, 32, advance_r)
+                update(pl.ds(pl.multiple_of(at, 32), 32), every)
+                update(pl.ds(pl.multiple_of(3 * h + at, 32), 32), every)
+                for shift in (h, 2 * h):
+                    update(pl.ds(pl.multiple_of(shift + at, 32), 32), top_h)
+                    update(pl.ds(pl.multiple_of(shift + at, 32), 32), end_h)
+            chunks(h, 32, advance_r)
 
         @pl.when(last)
         def _():
@@ -636,6 +650,7 @@
         cap = offsets.shape[2]
         h = side // 2
         mats = jnp.asarray(tables(side))
+        weights = pltpu.with_memory_space_constraint(weights, pltpu.HBM)
         block = jax.ShapeDtypeStruct((2, side, side), F32)
         hbm = pl.BlockSpec(memory_space=pltpu.HBM)
         smem = pl.BlockSpec(memory_space=pltpu.SMEM)
@@ -662,18 +677,18 @@
                 pltpu.VMEM((2, 2, h, side), F32),
                 pltpu.VMEM((2, 2, 2, h, side), F32),
                 [pltpu.VMEM((2, 2, h, side), F32) for _ in range(2)],
-                pltpu.VMEM((2, 2, 2, h, h), F32),
-                pltpu.VMEM((2, 2, 2, h, side), F32),
+                pltpu.VMEM((2, 2, STRIPS, side // STRIPS, h), F32),
+                pltpu.VMEM((2, 2, STRIPS, side // STRIPS, side), F32),
                 pltpu.VMEM((ITERS, n_row, 2, 128), F32),
                 pltpu.VMEM((ITERS, n_col, 2, 128), F32),
-                dma((48,)), dma((48,)), dma((2, 10)), dma((2, 10)),
+                dma((48 + 8 * STRIPS,)), dma((48 + 8 * STRIPS,)), dma((2, 6 + 2 * STRIPS)), dma((2, 6 + 2 * STRIPS)),
                 dma((ITERS, n_row)), dma((ITERS, n_row)),
                 dma((ITERS, n_col)), dma((ITERS, n_col)),
                 dma((4,)),
             ],
             compiler_params=pltpu.CompilerParams(
                 collective_id=0, has_side_effects=True, vmem_limit_bytes=53824 * 1024),
-        )(offsets[0, 0].T, counts, right_side, probe, weights, mats)
+        )(pltpu.with_memory_space_constraint(offsets[0, 0].T, pltpu.HBM), counts, right_side, probe, weights, mats)
 
     placed = (P(None, "row", "col"), P(), P(), P("row", "col", None, None), P("row", "col"))
     return jax.shard_map(

time: 83.6 us -> 81.7 us (0.977)
  local copies, waits for them, and re-layouts: 3.21 us -> 1.59 us
    unnamed x6 -> x2, local copies, waits for them, and re-layouts: 3.21 us -> 1.59 us
where the time goes in v4:
time: 81.7 us; the launch traced here: 80.4 us
  Pallas kernels  77.6 us (95%)
  local copies, waits for them, and re-layouts  1.59 us (2%)
  between operations  1.29 us (2%)
    pallas_call x1, Pallas kernels, local(): pl.pallas_call(functools.partial(kernel, n_row, n_col, n_x, cap, side), o...  77.6 us

profile of v4, /device:TPU:4, one launch (start us, length us, event | category | flops | bytes accessed | tf_op | source)
XLA Modules:
  0.0 80.4 jit_solution(906184573411049271)
XLA Ops:
  1.3 77.6 %shard_map.77 = (f32[2,256,256]{2,1,0:T(8,128)S(1)}, f32[2,256,256]{2,1,0:T(8,128)S(1)}) custom-call(s32[2,4]{1,0:T(2,128)} %bitcast.3, s32[1,1]{1,0:T(1,128)S(6)} %copy.10.cnt_ref, f32[2,256,256]{2,1,0:T(8,128)} %rhs_hbm.1, f32[2,256,256]{2,1,0:T(8,128)} %probe_hbm.1, f32[256,256]{1,0:T(8,128)} %w_hbm.1, bf16[8,256,256]{2,1,0:T(8,128)(2,1)} %constant.2.clone.mat_hbm), custom_call_target="tpu_custom_call" | custom-call | tf_op jit(solution)/shard_map/pallas_call | solution.py:661
  78.8 0.8 copy.11
  79.6 0.8 copy.12

commit v5 on v4

--- a/solution.py
+++ b/solution.py
@@ -495,9 +495,6 @@
                         chunks(h, 32, add)
                 begin(meet_x[c][p])
 
-        for key in pieces[:STRIPS]:
-            turn_z(*key)
-        turn_x(0)
         for copy in ones:
             copy.wait()
         total = T1[it, 0]
@@ -512,6 +509,9 @@
         ]
         for copy in twos:
             copy.start()
+        for key in pieces[:STRIPS]:
+            turn_z(*key)
+        turn_x(0)
         for key in pieces[STRIPS:]:
             turn_z(*key)
         turn_x(1)

time: 81.7 us -> 80.9 us (level); the launches traced: 80.4 us -> 80.5 us
  no operation moved by 1% of the time
where the time goes in v5:
time: 80.9 us; the launch traced here: 80.5 us
  Pallas kernels  77.7 us (96%)
  local copies, waits for them, and re-layouts  1.59 us (2%)
  between operations  1.29 us (2%)
    pallas_call x1, Pallas kernels, local(): pl.pallas_call(functools.partial(kernel, n_row, n_col, n_x, cap, side), o...  77.7 us

profile of v5, /device:TPU:4, one launch (start us, length us, event | category | flops | bytes accessed | tf_op | source)
XLA Modules:
  0.0 80.5 jit_solution(16621500400721810576)
XLA Ops:
  1.3 77.7 %shard_map.77 = (f32[2,256,256]{2,1,0:T(8,128)S(1)}, f32[2,256,256]{2,1,0:T(8,128)S(1)}) custom-call(s32[2,4]{1,0:T(2,128)} %bitcast.3, s32[1,1]{1,0:T(1,128)S(6)} %copy.10.cnt_ref, f32[2,256,256]{2,1,0:T(8,128)} %rhs_hbm.1, f32[2,256,256]{2,1,0:T(8,128)} %probe_hbm.1, f32[256,256]{1,0:T(8,128)} %w_hbm.1, bf16[8,256,256]{2,1,0:T(8,128)(2,1)} %constant.2.clone.mat_hbm), custom_call_target="tpu_custom_call" | custom-call | tf_op jit(solution)/shard_map/pallas_call | solution.py:661
  79.0 0.8 copy.11
  79.8 0.8 copy.12
